TPU v7x, 8 devices: a whole 2x2x1 slice. The times are simulated.
8 devices in a mesh: dz: 2 (over z, y), dy: 2 (over x), dx: 2 (over core).
Axes of the slice: x: 2, y: 2, z: 1, core: 2. Of those that a mesh axis runs over, the one named last changes fastest.
Arguments:
- x: bfloat16 [16384, 2048], P(('dx', 'dy', 'dz'))
- g: bfloat16 [16384, 2048], P(('dx', 'dy', 'dz'))
- w1: bfloat16 [2048, 8192], replicated
- w2: bfloat16 [8192, 2048], replicated
- w3: bfloat16 [2048, 8192], replicated
- w4: bfloat16 [8192, 2048], replicated
- m1: float32 [2048, 8192], P(('dx', 'dy', 'dz'))
- m2: float32 [8192, 2048], P(('dx', 'dy', 'dz'))
- m3: float32 [2048, 8192], P(('dx', 'dy', 'dz'))
- m4: float32 [8192, 2048], P(('dx', 'dy', 'dz'))
Outputs:
- output 1: bfloat16 [16384, 2048], P(('dx', 'dy', 'dz'))
- output 2: bfloat16 [2048, 8192], replicated
- output 3: bfloat16 [8192, 2048], replicated
- output 4: bfloat16 [2048, 8192], replicated
- output 5: bfloat16 [8192, 2048], replicated
- output 6: float32 [2048, 8192], P(('dx', 'dy', 'dz'))
- output 7: float32 [8192, 2048], P(('dx', 'dy', 'dz'))
- output 8: float32 [2048, 8192], P(('dx', 'dy', 'dz'))
- output 9: float32 [8192, 2048], P(('dx', 'dy', 'dz'))
All inputs are finite; a program needn't handle non-finite values.
Results may differ from a plain program's by a relative error of at most 0.010999.
Values are sent between devices in bfloat16 or wider.
A program may use at most 1.5 GiB of HBM per device.

v0:
```python
import jax
import jax.numpy as jnp
from jax import lax
from jax.sharding import PartitionSpec as P

LR = 0.0005
MU = 0.9
DATA = ("dx", "dy", "dz")


def _gelu(z):
    return jax.nn.gelu(z, approximate=True)


def _gelu_grad(z, dh):
    return jax.vjp(_gelu, z.astype(jnp.float32))[1](dh.astype(jnp.float32))[0]


def solution(mesh):
    ndy, ndz = mesh.shape["dy"], mesh.shape["dz"]
    n = mesh.shape["dx"] * ndy * ndz
    f32, bf = jnp.float32, jnp.bfloat16

    def reduce_scatter(s):
        for ax in DATA:
            s = lax.psum_scatter(s, ax, scatter_dimension=0, tiled=True)
        return s

    def all_gather(w):
        for ax in reversed(DATA):
            w = lax.all_gather(w, ax, axis=0, tiled=True)
        return w

    def update(w, m, s):
        idx = (lax.axis_index("dx") * ndy + lax.axis_index("dy")) * ndz + lax.axis_index("dz")
        rows = m.shape[0]
        w_loc = lax.dynamic_slice_in_dim(w, idx * rows, rows, 0).astype(f32)
        m_new = MU * m + s / n
        return all_gather((w_loc - LR * m_new).astype(bf)), m_new

    def local(x, g, w1, w2, w3, w4, m1, m2, m3, m4):
        z1 = jnp.dot(x, w1, preferred_element_type=f32).astype(bf)
        h1 = _gelu(z1.astype(f32)).astype(bf)
        h2 = (jnp.dot(h1, w2, preferred_element_type=f32) + x.astype(f32)).astype(bf)
        z3 = jnp.dot(h2, w3, preferred_element_type=f32).astype(bf)
        h3 = _gelu(z3.astype(f32)).astype(bf)
        s4 = reduce_scatter(jnp.dot(h3.T, g, preferred_element_type=f32))
        dh3 = jnp.dot(g, w4.T, preferred_element_type=f32).astype(bf)
        dz3 = _gelu_grad(z3, dh3).astype(bf)
        s3 = reduce_scatter(jnp.dot(h2.T, dz3, preferred_element_type=f32))
        dh2 = (jnp.dot(dz3, w3.T, preferred_element_type=f32) + g.astype(f32)).astype(bf)
        s2 = reduce_scatter(jnp.dot(h1.T, dh2, preferred_element_type=f32))
        dh1 = jnp.dot(dh2, w2.T, preferred_element_type=f32).astype(bf)
        dz1 = _gelu_grad(z1, dh1).astype(bf)
        s1 = reduce_scatter(jnp.dot(x.T, dz1, preferred_element_type=f32))
        dx = (jnp.dot(dz1, w1.T, preferred_element_type=f32) + dh2.astype(f32)).astype(bf)
        w4n, m4n = update(w4, m4, s4)
        w3n, m3n = update(w3, m3, s3)
        w2n, m2n = update(w2, m2, s2)
        w1n, m1n = update(w1, m1, s1)
        return (dx, w1n, w2n, w3n, w4n, m1n, m2n, m3n, m4n)

    row, rep = P(DATA, None), P()
    return jax.shard_map(local, mesh=mesh,
                         in_specs=(row, row, rep, rep, rep, rep, row, row, row, row),
                         out_specs=(row, rep, rep, rep, rep, row, row, row, row),
                         check_vma=False)
```

profile of v0, /device:TPU:0, one launch (start us, length us, event | category | flops | bytes accessed | tf_op | source)
XLA Modules:
  0.0 4694.0 jit_solution(18109150769010027868)
XLA Ops:
  7.2 77.9 %convolution_convert_fusion.1 = bf16[2048,8192]{1,0:T(8,128)(2,1)} fusion(bf16[2048,2048]{1,0:T(8,128)(2,1)} %param.10, bf16[2048,8192]{1,0:T(8,128)(2,1)} %param.12), kind=kOutput, calls=%fused_computation.41 | convolution fusion | flops 68736253952 | bytes 75497472 | tf_op jit(solution)/shard_map/dot_general | solution.py:42
  85.2 92.0 %add_convert_fusion.2 = bf16[2048,2048]{1,0:T(8,128)(2,1)} fusion(bf16[2048,2048]{1,0:T(8,128)(2,1)} %param.10, bf16[8192,2048]{1,0:T(8,128)(2,1)} %param.13, bf16[2048,8192]{1,0:T(8,128)(2,1)} %convolution_convert_fusion.1), kind=kOutput, calls=%fused_computation.44 | convolution fusion | flops 68899831808 | bytes 83886080 | tf_op jit(solution)/shard_map/dot_general | solution.py:44
  177.2 78.1 %convolution_convert_fusion = bf16[2048,8192]{1,0:T(8,128)(2,1)} fusion(bf16[2048,2048]{1,0:T(8,128)(2,1)} %add_convert_fusion.2, bf16[2048,8192]{1,0:T(8,128)(2,1)} %param.14), kind=kOutput, calls=%fused_computation.40 | convolution fusion | flops 68736253952 | bytes 75497472 | tf_op jit(solution)/shard_map/dot_general | solution.py:45
  255.3 121.3 %fusion.4 = bf16[2048,8192]{1,0:T(8,128)(2,1)} fusion(bf16[2048,8192]{1,0:T(8,128)(2,1)} %convolution_convert_fusion, bf16[2048,2048]{1,0:T(8,128)(2,1)} %param.11, bf16[8192,2048]{1,0:T(8,128)(2,1)} %param.15), kind=kOutput, calls=%fused_computation.16 | convolution fusion | flops 69105352704 | bytes 109051904 | tf_op jit(solution)/shard_map/dot_general | solution.py:48
  376.5 79.5 %fusion.35 = f32[2048,8192]{0,1:T(8,128)} fusion(bf16[2048,2048]{1,0:T(8,128)(2,1)} %add_convert_fusion.2, bf16[2048,8192]{1,0:T(8,128)(2,1)} %fusion.4), kind=kOutput, calls=%fused_computation.60 | convolution fusion | flops 68719476736 | bytes 109051904 | tf_op jit(solution)/shard_map/dot_general | solution.py:50
  456.1 81.4 %add_convert_fusion.1 = bf16[2048,2048]{1,0:T(8,128)(2,1)} fusion(bf16[2048,2048]{1,0:T(8,128)(2,1)} %param.11, bf16[2048,8192]{1,0:T(8,128)(2,1)} %fusion.4, bf16[2048,8192]{1,0:T(8,128)(2,1)} %param.14), kind=kOutput, calls=%fused_computation.43 | convolution fusion | flops 68732059648 | bytes 83886080 | tf_op jit(solution)/shard_map/dot_general | solution.py:51
  537.5 93.1 %fusion.32 = f32[8192,2048]{1,0:T(8,128)} fusion(bf16[2048,2048]{1,0:T(8,128)(2,1)} %add_convert_fusion.1, bf16[2048,8192]{1,0:T(8,128)(2,1)} %convolution_convert_fusion.1), kind=kOutput, calls=%fused_computation.59 | convolution fusion | flops 68887248896 | bytes 109051904 | tf_op jit(solution)/shard_map/dot_general | solution.py:52
  630.6 121.3 %fusion.7 = bf16[2048,8192]{1,0:T(8,128)(2,1)} fusion(bf16[2048,8192]{1,0:T(8,128)(2,1)} %convolution_convert_fusion.1, bf16[2048,2048]{1,0:T(8,128)(2,1)} %add_convert_fusion.1, bf16[8192,2048]{1,0:T(8,128)(2,1)} %param.13), kind=kOutput, calls=%fused_computation.19 | convolution fusion | flops 69105352704 | bytes 109051904 | tf_op jit(solution)/shard_map/dot_general | solution.py:53
  751.9 79.6 %convolution_bitcast_fusion = f32[2048,8192]{0,1:T(8,128)} fusion(bf16[2048,8192]{1,0:T(8,128)(2,1)} %fusion.7, bf16[2048,2048]{1,0:T(8,128)(2,1)} %param.10), kind=kOutput, calls=%fused_computation.34 | convolution fusion | flops 68719476736 | bytes 109051904 | tf_op jit(solution)/shard_map/dot_general | solution.py:55
  831.6 93.1 %fusion.22 = f32[8192,2048]{1,0:T(8,128)} fusion(bf16[2048,2048]{1,0:T(8,128)(2,1)} %param.11, bf16[2048,8192]{1,0:T(8,128)(2,1)} %convolution_convert_fusion), kind=kOutput, calls=%fused_computation.35 | convolution fusion | flops 68887248896 | bytes 109051904 | tf_op jit(solution)/shard_map/dot_general | solution.py:47
  924.8 0.5 reduce-scatter.27.cloned.1.call-update
  925.9 0.7 reduce-scatter.15.cloned.1.call-update
  926.6 75.0 %reduce-scatter.31.cloned.1.call-done = f32[4096,2048]{1,0:T(8,128)} async-done(((f32[8192,2048]{1,0:T(8,128)}), f32[4096,2048]{1,0:T(8,128)}) %reduce-scatter.31.cloned.1.call-update) | async-done | bytes 33554448 | tf_op jit(solution)/shard_map/reduce_scatter | solution.py:26
  1001.7 369.3 %reduce-scatter.27.cloned.1.call-done = f32[512,8192]{0,1:T(8,128)} async-done(((f32[1024,8192]{0,1:T(8,128)}), f32[512,8192]{0,1:T(8,128)}) %reduce-scatter.27.cloned.1.call-update) | async-done | bytes 16777232 | tf_op jit(solution)/shard_map/reduce_scatter | solution.py:26
  1371.1 368.2 %reduce-scatter.21.cloned.1.call-done = f32[2048,2048]{1,0:T(8,128)} async-done(((f32[4096,2048]{1,0:T(8,128)}), f32[2048,2048]{1,0:T(8,128)}) %reduce-scatter.21.cloned.1.call-update) | async-done | bytes 16777232 | tf_op jit(solution)/shard_map/reduce_scatter | solution.py:26
  1739.3 368.3 %reduce-scatter.15.cloned.1.call-done = f32[512,8192]{0,1:T(8,128)} async-done(((f32[1024,8192]{0,1:T(8,128)}), f32[512,8192]{0,1:T(8,128)}) %reduce-scatter.15.cloned.1.call-update) | async-done | bytes 16777232 | tf_op jit(solution)/shard_map/reduce_scatter | solution.py:26
  2107.7 368.3 %reduce-scatter.33.cloned.1.call-done = f32[2048,2048]{1,0:T(8,128)} async-done(((f32[4096,2048]{1,0:T(8,128)}), f32[2048,2048]{1,0:T(8,128)}) %reduce-scatter.33.cloned.1.call-update) | async-done | bytes 16777232 | tf_op jit(solution)/shard_map/reduce_scatter | solution.py:26
  2476.1 4.6 constant_dynamic-slice_fusion
  2480.8 6.4 copy.30
  2487.2 9.0 copy.22
  2496.1 168.5 %reduce-scatter.29.cloned.1.call-done = f32[256,8192]{0,1:T(8,128)} async-done(((f32[512,8192]{0,1:T(8,128)}), f32[256,8192]{0,1:T(8,128)}) %reduce-scatter.29.cloned.1.call-update) | async-done | bytes 8388624 | tf_op jit(solution)/shard_map/reduce_scatter | solution.py:26
  2664.7 13.0 subtract_convert_fusion.1
  2677.7 175.4 %reduce-scatter.23.cloned.1.call-done = f32[1024,2048]{1,0:T(8,128)} async-done(((f32[2048,2048]{1,0:T(8,128)}), f32[1024,2048]{1,0:T(8,128)}) %reduce-scatter.23.cloned.1.call-update) | async-done | bytes 8388624 | tf_op jit(solution)/shard_map/reduce_scatter | solution.py:26
  2853.2 12.6 subtract_convert_fusion.2
  2865.8 4.6 constant_dynamic-slice_fusion.1
  2870.4 6.4 copy.29
  2876.8 9.0 copy.20
  2885.8 156.0 %reduce-scatter.17.cloned.1.call-done = f32[256,8192]{0,1:T(8,128)} async-done(((f32[512,8192]{0,1:T(8,128)}), f32[256,8192]{0,1:T(8,128)}) %reduce-scatter.17.cloned.1.call-update) | async-done | bytes 8388624 | tf_op jit(solution)/shard_map/reduce_scatter | solution.py:26
  3041.8 12.9 subtract_convert_fusion.3
  3054.8 175.5 %reduce-scatter.35.cloned.1.call-done = f32[1024,2048]{1,0:T(8,128)} async-done(((f32[2048,2048]{1,0:T(8,128)}), f32[1024,2048]{1,0:T(8,128)}) %reduce-scatter.35.cloned.1.call-update) | async-done | bytes 8388624 | tf_op jit(solution)/shard_map/reduce_scatter | solution.py:26
  3230.3 12.2 subtract_convert_fusion
  3242.5 91.5 %all-gather.25.cloned.1.call-done = bf16[512,8192]{0,1:T(8,128)(2,1)} async-done(((bf16[256,8192]{0,1:T(8,128)(2,1)}), bf16[512,8192]{0,1:T(8,128)(2,1)}) %all-gather.25.cloned.1.call-update) | async-done | bytes 8388624 | tf_op jit(solution)/shard_map/all_gather | solution.py:31
  3334.1 104.2 %all-gather.19.cloned.1.call-done = bf16[2048,2048]{1,0:T(8,128)(2,1)} async-done(((bf16[1024,2048]{1,0:T(8,128)(2,1)}), bf16[2048,2048]{1,0:T(8,128)(2,1)}) %all-gather.19.cloned.1.call-update) | async-done | bytes 8388624 | tf_op jit(solution)/shard_map/all_gather | solution.py:31
  3438.3 104.1 %all-gather.13.cloned.1.call-done = bf16[512,8192]{0,1:T(8,128)(2,1)} async-done(((bf16[256,8192]{0,1:T(8,128)(2,1)}), bf16[512,8192]{0,1:T(8,128)(2,1)}) %all-gather.13.cloned.1.call-update) | async-done | bytes 8388624 | tf_op jit(solution)/shard_map/all_gather | solution.py:31
  3542.5 104.2 %all-gather.31.cloned.1.call-done = bf16[2048,2048]{1,0:T(8,128)(2,1)} async-done(((bf16[1024,2048]{1,0:T(8,128)(2,1)}), bf16[2048,2048]{1,0:T(8,128)(2,1)}) %all-gather.31.cloned.1.call-update) | async-done | bytes 8388624 | tf_op jit(solution)/shard_map/all_gather | solution.py:31
  3646.8 198.0 %all-gather.27.cloned.1.call-done = bf16[1024,8192]{0,1:T(8,128)(2,1)} async-done(((bf16[512,8192]{0,1:T(8,128)(2,1)}), bf16[1024,8192]{0,1:T(8,128)(2,1)}) %all-gather.27.cloned.1.call-update) | async-done | bytes 16777232 | tf_op jit(solution)/shard_map/all_gather | solution.py:31
  3844.9 198.0 %all-gather.21.cloned.1.call-done = bf16[4096,2048]{1,0:T(8,128)(2,1)} async-done(((bf16[2048,2048]{1,0:T(8,128)(2,1)}), bf16[4096,2048]{1,0:T(8,128)(2,1)}) %all-gather.21.cloned.1.call-update) | async-done | bytes 16777232 | tf_op jit(solution)/shard_map/all_gather | solution.py:31
  4042.9 198.2 %all-gather.15.cloned.1.call-done = bf16[1024,8192]{0,1:T(8,128)(2,1)} async-done(((bf16[512,8192]{0,1:T(8,128)(2,1)}), bf16[1024,8192]{0,1:T(8,128)(2,1)}) %all-gather.15.cloned.1.call-update) | async-done | bytes 16777232 | tf_op jit(solution)/shard_map/all_gather | solution.py:31
  4241.2 198.0 %all-gather.33.cloned.1.call-done = bf16[4096,2048]{1,0:T(8,128)(2,1)} async-done(((bf16[2048,2048]{1,0:T(8,128)(2,1)}), bf16[4096,2048]{1,0:T(8,128)(2,1)}) %all-gather.33.cloned.1.call-update) | async-done | bytes 16777232 | tf_op jit(solution)/shard_map/all_gather | solution.py:31
  4439.2 81.2 %add_convert_fusion = bf16[2048,2048]{1,0:T(8,128)(2,1)} fusion(bf16[2048,2048]{1,0:T(8,128)(2,1)} %add_convert_fusion.1, bf16[2048,8192]{1,0:T(8,128)(2,1)} %fusion.7, bf16[2048,8192]{1,0:T(8,128)(2,1)} %param.12), kind=kOutput, calls=%fused_computation.42 | convolution fusion | flops 68732059648 | bytes 83886080 | tf_op jit(solution)/shard_map/dot_general | solution.py:56
  4520.5 8.9 copy.27
  4529.4 8.9 copy.26
  4538.2 40.5 copy.25
  4578.8 11.7 all-gather.17.cloned.1.call-done
  4590.5 40.5 copy.24
  4631.0 10.2 all-gather.35.cloned.1.call-done
  4641.2 22.9 copy.33
  4664.1 22.9 copy.34
  (51 shorter events, 1.8 us)
Async XLA Ops:
  7.2 917.6 %reduce-scatter.25.cloned.1.call-start = ((), (), s32[]{:S(2)}) async-start(), calls=%async_computation.24 | async-start | bytes 100663296 | tf_op jit(solution)/shard_map/reduce_scatter | solution.py:26
  456.0 469.3 %reduce-scatter.19.cloned.1.call-start = ((), (), s32[]{:S(2)}) async-start(), calls=%async_computation.18 | async-start | bytes 100663296 | tf_op jit(solution)/shard_map/reduce_scatter | solution.py:26
  630.6 295.3 %reduce-scatter.13.cloned.1.call-start = ((), (), s32[]{:S(2)}) async-start(), calls=%async_computation.12 | async-start | bytes 100663296 | tf_op jit(solution)/shard_map/reduce_scatter | solution.py:26
  831.5 170.1 %reduce-scatter.31.cloned.1.call-start = ((), (), s32[]{:S(2)}) async-start(), calls=%async_computation.30 | async-start | bytes 100663296 | tf_op jit(solution)/shard_map/reduce_scatter | solution.py:26
  924.7 446.4 %reduce-scatter.27.cloned.1.call-start = ((), (), s32[]{:S(2)}) async-start(), calls=%async_computation.25 | async-start | bytes 50331648 | tf_op jit(solution)/shard_map/reduce_scatter | solution.py:26
  925.3 814.0 %reduce-scatter.21.cloned.1.call-start = ((), (), s32[]{:S(2)}) async-start(), calls=%async_computation.19 | async-start | bytes 50331648 | tf_op jit(solution)/shard_map/reduce_scatter | solution.py:26
  925.8 1181.8 %reduce-scatter.15.cloned.1.call-start = ((), (), s32[]{:S(2)}) async-start(), calls=%async_computation.13 | async-start | bytes 50331648 | tf_op jit(solution)/shard_map/reduce_scatter | solution.py:26
  926.6 1549.5 %reduce-scatter.33.cloned.1.call-start = ((), (), s32[]{:S(2)}) async-start(), calls=%async_computation.31 | async-start | bytes 50331648 | tf_op jit(solution)/shard_map/reduce_scatter | solution.py:26
  1001.7 1663.0 %reduce-scatter.29.cloned.1.call-start = ((), (), s32[]{:S(2)}) async-start(), calls=%async_computation.26 | async-start | bytes 25165824 | tf_op jit(solution)/shard_map/reduce_scatter | solution.py:26
  1371.1 1482.1 %reduce-scatter.23.cloned.1.call-start = ((), (), s32[]{:S(2)}) async-start(), calls=%async_computation.20 | async-start | bytes 25165824 | tf_op jit(solution)/shard_map/reduce_scatter | solution.py:26
  1739.3 1302.5 %reduce-scatter.17.cloned.1.call-start = ((), (), s32[]{:S(2)}) async-start(), calls=%async_computation.14 | async-start | bytes 25165824 | tf_op jit(solution)/shard_map/reduce_scatter | solution.py:26
  2107.7 1122.6 %reduce-scatter.35.cloned.1.call-start = ((), (), s32[]{:S(2)}) async-start(), calls=%async_computation.32 | async-start | bytes 25165824 | tf_op jit(solution)/shard_map/reduce_scatter | solution.py:26
  2476.1 857.9 %all-gather.25.cloned.1.call-start = ((), (), s32[]{:S(2)}) async-start(), calls=%async_computation.27 | async-start | bytes 12582912 | tf_op jit(solution)/shard_map/all_gather | solution.py:31
  2677.7 760.6 %all-gather.19.cloned.1.call-start = ((), (), s32[]{:S(2)}) async-start(), calls=%async_computation.21 | async-start | bytes 12582912 | tf_op jit(solution)/shard_map/all_gather | solution.py:31
  2865.8 676.7 %all-gather.13.cloned.1.call-start = ((), (), s32[]{:S(2)}) async-start(), calls=%async_computation.15 | async-start | bytes 12582912 | tf_op jit(solution)/shard_map/all_gather | solution.py:31
  3054.7 592.0 %all-gather.31.cloned.1.call-start = ((), (), s32[]{:S(2)}) async-start(), calls=%async_computation.33 | async-start | bytes 12582912 | tf_op jit(solution)/shard_map/all_gather | solution.py:31
  3242.5 602.3 %all-gather.27.cloned.1.call-start = ((), (), s32[]{:S(2)}) async-start(), calls=%async_computation.28 | async-start | bytes 25165824 | tf_op jit(solution)/shard_map/all_gather | solution.py:31
  3334.1 708.8 %all-gather.21.cloned.1.call-start = ((), (), s32[]{:S(2)}) async-start(), calls=%async_computation.22 | async-start | bytes 25165824 | tf_op jit(solution)/shard_map/all_gather | solution.py:31
  3438.3 802.8 %all-gather.15.cloned.1.call-start = ((), (), s32[]{:S(2)}) async-start(), calls=%async_computation.16 | async-start | bytes 25165824 | tf_op jit(solution)/shard_map/all_gather | solution.py:31
  3542.5 896.7 %all-gather.33.cloned.1.call-start = ((), (), s32[]{:S(2)}) async-start(), calls=%async_computation.34 | async-start | bytes 25165824 | tf_op jit(solution)/shard_map/all_gather | solution.py:31
  3646.7 891.5 %all-gather.29.cloned.1.call-start = ((), (), s32[]{:S(2)}) async-start(), calls=%async_computation.29 | async-start | bytes 50331648 | tf_op jit(solution)/shard_map/all_gather | solution.py:31
  3844.8 733.9 %all-gather.23.cloned.1.call-start = ((), (), s32[]{:S(2)}) async-start(), calls=%async_computation.23 | async-start | bytes 50331648 | tf_op jit(solution)/shard_map/all_gather | solution.py:31
  4042.9 547.6 %all-gather.17.cloned.1.call-start = ((), (), s32[]{:S(2)}) async-start(), calls=%async_computation.17 | async-start | bytes 50331648 | tf_op jit(solution)/shard_map/all_gather | solution.py:31
  4241.1 400.0 %all-gather.35.cloned.1.call-start = ((), (), s32[]{:S(2)}) async-start(), calls=%async_computation.35 | async-start | bytes 50331648 | tf_op jit(solution)/shard_map/all_gather | solution.py:31
Sparse Core Ops, SparseCore 0:
  456.2 76.7 reduce-scatter.24
  630.7 76.7 reduce-scatter.18
  831.7 76.7 reduce-scatter.12
  924.8 76.7 reduce-scatter.30
  1003.7 367.2 reduce-scatter.26
  1373.1 366.0 reduce-scatter.20
  1741.5 366.0 reduce-scatter.14
  2109.9 366.0 reduce-scatter.32
  2478.3 186.2 reduce-scatter.28
  2666.8 186.3 reduce-scatter.22
  2855.4 186.2 reduce-scatter.16
  3043.9 186.3 reduce-scatter.34
  3231.8 102.2 all-gather.24
  3336.0 102.2 all-gather.18
  3440.2 102.2 all-gather.12
  3544.4 102.2 all-gather.30
  3648.1 196.6 all-gather.26
  3846.2 196.6 all-gather.20
  4044.4 196.6 all-gather.14
  4242.5 196.6 all-gather.32
  4440.7 48.0 all-gather.28
  4490.4 49.2 all-gather.22
  4541.2 49.2 all-gather.16
  4591.9 49.2 all-gather.34
where the time goes:
time: 4700 us; the launch traced here: 4690 us
  waiting for transfers between devices  3440 us (73%)
  matrix products  998 us (21%)
  local copies, waits for them, and re-layouts  185 us (4%)
  other arithmetic  50.7 us (1%)
    reduce_scatter x12, waiting for transfers between devices, reduce_scatter(): s = lax.psum_scatter(s, ax, scatter_dimension=0, tiled=True)  2220 us
    all_gather x12, waiting for transfers between devices, all_gather(): w = lax.all_gather(w, ax, axis=0, tiled=True)  1220 us
    unnamed x10, local copies, waits for them, and re-layouts  175 us
    dot_general x1, matrix products, local(): dh3 = jnp.dot(g, w4.T, preferred_element_type=f32).astype(bf)  121 us
    dot_general x1, matrix products, local(): dh1 = jnp.dot(dh2, w2.T, preferred_element_type=f32).astype(bf)  121 us
  transfers between devices with their start and end apart: 24, of which 19 were waited for; matrix products, arithmetic and copies ran while one was open for 16% of the time, Pallas kernels for 0%

commit v1 on v0

v1 whole, which is shorter than its diff:
```python
import jax
import jax.numpy as jnp
from jax import lax
from jax.experimental import pallas as pl
from jax.experimental.layout import Layout, with_layout_constraint
from jax.sharding import PartitionSpec as P


LR = 0.0005
MU = 0.9
DATA = ("dx", "dy", "dz")


def _gelu(z):
    return jax.nn.gelu(z, approximate=True)


def _gelu_grad(z, dh):
    return jax.vjp(_gelu, z.astype(jnp.float32))[1](dh.astype(jnp.float32))[0]


def _row_major(a):
    return with_layout_constraint(a, Layout(major_to_minor=(0, 1)))


def _copy_block(src, dst):
    dst[...] = src[...]


def _copy(a):
    r, c = a.shape
    spec = pl.BlockSpec(((1 << 20) // c, c), lambda b: (b, 0))
    return pl.pallas_call(_copy_block, grid=(r * c >> 20,), in_specs=[spec], out_specs=spec,
                          out_shape=jax.ShapeDtypeStruct(a.shape, a.dtype),
                          cost_estimate=pl.CostEstimate(flops=r * c, bytes_accessed=4 * r * c, transcendentals=0))(a)


def solution(mesh):
    ndx, ndy, ndz = mesh.shape["dx"], mesh.shape["dy"], mesh.shape["dz"]
    n = ndx * ndy * ndz
    f32, bf = jnp.float32, jnp.bfloat16
    swap = [(0, 1), (1, 0)]

    def nt(a, b):
        return lax.dot_general(a, b, (((1,), (1,)), ((), ())), preferred_element_type=f32)

    def tn(a, b):
        return lax.dot_general(a, b, (((0,), (0,)), ((), ())), preferred_element_type=f32)

    def nn(a, b):
        return jnp.dot(a, b, preferred_element_type=f32)

    def act(z):
        return _gelu(z.astype(f32)).astype(bf)

    def body(x, g, w1, w2, w3, w4, m1, m2, m3, m4):
        i, j, k = lax.axis_index("dx"), lax.axis_index("dy"), lax.axis_index("dz")
        q, qp = 2 * i + j, 2 * (1 - i) + j
        d, f = w1.shape
        fq = f // 4

        def cols(a, b):
            return lax.dynamic_slice_in_dim(a, b * fq, fq, 1)

        def rows(a, b):
            return lax.dynamic_slice_in_dim(a, b * fq, fq, 0)

        def send(a, ax):
            return lax.ppermute(a, ax, swap)

        def both(a):
            return lax.all_gather(a, "dx", axis=0, tiled=True)

        def sum_f(s):
            half = fq // 2
            r = send(lax.dynamic_slice_in_dim(s, (1 - k) * half, half, 0), "dz")
            return lax.dynamic_slice_in_dim(s, k * half, half, 0) + r

        def sum_d(s):
            s = s.reshape(4, 2, d // 8, fq)
            r = send(lax.dynamic_index_in_dim(s, 1 - k, 1, keepdims=False), "dz")
            s = lax.dynamic_index_in_dim(s, k, 1, keepdims=False) + r
            parts = []
            for t in range(4):
                part = lax.dynamic_index_in_dim(s, q ^ t, 0, keepdims=False)
                if t:
                    part = lax.ppermute(part, ("dy", "dx"), [(a, a ^ (0, 2, 1, 3)[t]) for a in range(4)])
                parts.append(part)
            parts = [jnp.where(j == 0, parts[b], parts[b ^ 1]) for b in range(4)]
            return jnp.concatenate([jnp.where(i == 0, parts[b], parts[b ^ 2]) for b in range(4)], axis=1)

        def update(w, m, s, l):
            rws = m.shape[0]
            w_loc = lax.dynamic_slice_in_dim(w, (q * 2 + k) * rws, rws, 0).astype(f32)
            m_new = _row_major(MU * m + s / n)
            w_new = _row_major((w_loc - LR * m_new).astype(bf))
            if l > 2:
                w_new = lax.all_gather(w_new, "dz", axis=0, tiled=True)
                w_new = lax.all_gather(w_new, ("dx", "dy"), axis=0, tiled=True)
            else:
                w_new = lax.all_gather(w_new, DATA, axis=0, tiled=True)
            return _copy(w_new), m_new

        g_x = send(g, "dy")
        g_p = send(g, "dx")
        x_x = send(x, "dy")
        x_p = send(x, "dx")
        z1 = nn(x, w1).astype(bf)
        h1 = act(z1)
        h2 = (nn(h1, w2) + x.astype(f32)).astype(bf)
        h2_x = send(h2, "dy")
        h2_p = send(h2, "dx")
        h1_r = send(cols(h1, qp), "dx")
        g_o = both(g_x)
        h2_o = both(h2_x)
        x_o = both(x_x)
        z3 = nn(h2, w3).astype(bf)
        h3 = act(z3)
        h3_r = send(cols(h3, qp), "dx")
        dz3 = _gelu_grad(z3, nt(g, w4).astype(bf)).astype(bf)
        dz3_r = send(cols(dz3, qp), "dx")
        s4 = tn(cols(h3, q), g) + tn(h3_r, g_p)
        z3_o = nn(h2_o, cols(w3, q)).astype(bf)
        h3_o = act(z3_o)
        s4 = s4 + tn(h3_o, g_o)
        s4 = sum_f(s4)
        dz3_o = _gelu_grad(z3_o, nt(g_o, rows(w4, q)).astype(bf)).astype(bf)
        s3 = tn(h2, cols(dz3, q)) + tn(h2_p, dz3_r)
        s3 = s3 + tn(h2_o, dz3_o)
        s3 = sum_d(s3)
        dh2 = (nt(dz3, w3) + g.astype(f32)).astype(bf)
        dh2_x = send(dh2, "dy")
        dh2_p = send(dh2, "dx")
        dh2_o = both(dh2_x)
        w4n, m4n = update(w4, m4, s4, 4)
        dz1 = _gelu_grad(z1, nt(dh2, w2).astype(bf)).astype(bf)
        dz1_r = send(cols(dz1, qp), "dx")
        w3n, m3n = update(w3, m3, s3, 3)
        z1_o = nn(x_o, cols(w1, q)).astype(bf)
        h1_o = act(z1_o)
        s1 = tn(x, cols(dz1, q)) + tn(x_p, dz1_r)
        dz1_o = _gelu_grad(z1_o, nt(dh2_o, rows(w2, q)).astype(bf)).astype(bf)
        s1 = s1 + tn(x_o, dz1_o)
        s1 = sum_d(s1)
        s2 = tn(cols(h1, q), dh2) + tn(h1_r, dh2_p)
        s2 = s2 + tn(h1_o, dh2_o)
        s2 = sum_f(s2)
        w1n, m1n = update(w1, m1, s1, 1)
        w2n, m2n = update(w2, m2, s2, 2)
        dx = (nt(dz1, w1) + dh2.astype(f32)).astype(bf)
        return (dx, w1n, w2n, w3n, w4n, m1n, m2n, m3n, m4n)

    row, rep = P(DATA, None), P()
    return jax.shard_map(body, mesh=mesh,
                         in_specs=(row, row, rep, rep, rep, rep, row, row, row, row),
                         out_specs=(row, rep, rep, rep, rep, row, row, row, row),
                         check_vma=False)
```

time: 4700 us -> 3150 us (0.67)
  waiting for transfers between devices: 3440 us -> 1550 us
  matrix products: 998 us -> 1300 us
  local copies, waits for them, and re-layouts: 185 us -> 71.9 us
  Pallas kernels: 0 us -> 111 us
    reduce_scatter x12 -> x0, waiting for transfers between devices: 2220 us -> none  [reduce_scatter(): s = lax.psum_scatter(s, ax, scatter_dimension=0, tiled=True)]
    ppermute x0 -> x22, waiting for transfers between devices: none -> 1360 us  [the longest x16 1270 us: send(): return lax.ppermute(a, ax, swap)]
    all_gather x12 -> x10, waiting for transfers between devices: 1220 us -> 186 us  [the longest x2 171 us: update(): w_new = lax.all_gather(w_new, ('dx', 'dy'), axis=0, tiled=True)]
    dot_general x11 -> x23, matrix products: 998 us -> 1300 us  [the longest x6 498 us: nt(): lax.dot_general(a, b, (((1,), (1,)), ((), ())), preferred_element_type=f32)]
    unnamed x10 -> x14, local copies, waits for them, and re-layouts: 175 us -> 0.03 us
    pallas_call x0 -> x4, Pallas kernels: none -> 111 us  [_copy(): pl.pallas_call(_copy_block, grid=(r * c >> 20,), in_specs=[spec], out_spe...]
  transfers between devices with their start and end apart: 24 -> 32, of which waited for: 19 -> 13; matrix products, arithmetic and copies ran while one was open for 16% -> 40% of each run, Pallas kernels for 0% -> 3%
where the time goes in v1:
time: 3150 us; the launch traced here: 3140 us
  waiting for transfers between devices  1550 us (49%)
  matrix products  1300 us (41%)
  Pallas kernels  111 us (4%)
  other arithmetic  85.2 us (3%)
  local copies, waits for them, and re-layouts  71.9 us (2%)
    ppermute x16, waiting for transfers between devices, send(): return lax.ppermute(a, ax, swap)  1270 us
    dot_general x6, matrix products, nt(): lax.dot_general(a, b, (((1,), (1,)), ((), ())), preferred_element_type=f32)  498 us
    dot_general x12, matrix products, tn(): lax.dot_general(a, b, (((0,), (0,)), ((), ())), preferred_element_type=f32)  435 us
    dot_general x5, matrix products, nn(): return jnp.dot(a, b, preferred_element_type=f32)  367 us
    all_gather x2, waiting for transfers between devices, update(): w_new = lax.all_gather(w_new, ('dx', 'dy'), axis=0, tiled=True)  171 us
    pallas_call x4, Pallas kernels, _copy(): pl.pallas_call(_copy_block, grid=(r * c >> 20,), in_specs=[spec], out_spe...  111 us
    ppermute x6, waiting for transfers between devices, sum_d(): lax.ppermute(part, ('dy', 'dx'), [(a, a ^ (0, 2, 1, 3)[t]) for a in range...  90.8 us
  transfers between devices with their start and end apart: 32, of which 13 were waited for; matrix products, arithmetic and copies ran while one was open for 40% of the time, Pallas kernels for 3%

profile of v1, /device:TPU:0, one launch (start us, length us, event | category | flops | bytes accessed | tf_op | source)
XLA Modules:
  0.0 3144.8 jit_solution(4018505112649782041)
XLA Ops:
  7.2 94.2 %fusion.13 = (bf16[2048,8192]{1,0:T(8,128)(2,1)}, bf16[2048,8192]{1,0:T(8,128)(2,1)}) fusion(bf16[2048,2048]{1,0:T(8,128)(2,1)} %param.10, bf16[2048,8192]{1,0:T(8,128)(2,1)} %param.12), kind=kOutput, calls=%fused_computation.25 | convolution fusion | flops 68904026112 | bytes 109051904 | tf_op jit(solution)/shard_map/dot_general | solution.py:51
  101.5 92.0 %add_convert_fusion.2 = bf16[2048,2048]{1,0:T(8,128)(2,1)} fusion(bf16[2048,2048]{1,0:T(8,128)(2,1)} %param.10, bf16[8192,2048]{1,0:T(8,128)(2,1)} %param.13, bf16[2048,8192]{1,0:T(8,128)(2,1)} %get-tuple-element.32), kind=kOutput, calls=%fused_computation.75 | convolution fusion | flops 68899831808 | bytes 83886080 | tf_op jit(solution)/shard_map/dot_general | solution.py:51
  196.7 180.8 %collective-permute-done.13 = bf16[2048,2048]{1,0:T(8,128)(2,1)} collective-permute-done((bf16[2048,2048]{1,0:T(8,128)(2,1)}, bf16[2048,2048]{1,0:T(8,128)(2,1)}, u32[]{:S(2)}, u32[]{:S(2)}) %collective-permute-start.13) | collective-permute-done | bytes 8388640 | tf_op jit(solution)/shard_map/ppermute | solution.py:69
  379.6 96.8 %fusion.21 = (bf16[2048,8192]{1,0:T(8,128)(2,1)}, bf16[2048,8192]{1,0:T(8,128)(2,1)}) fusion(bf16[2048,2048]{1,0:T(8,128)(2,1)} %add_convert_fusion.2, bf16[2048,8192]{1,0:T(8,128)(2,1)} %param.14), kind=kOutput, calls=%fused_computation.33 | convolution fusion | flops 68904026112 | bytes 109051904 | tf_op jit(solution)/shard_map/dot_general | solution.py:51
  476.4 262.9 %collective-permute-done.14 = bf16[2048,2048]{1,0:T(8,128)(2,1)} collective-permute-done((bf16[2048,2048]{1,0:T(8,128)(2,1)}, bf16[2048,2048]{1,0:T(8,128)(2,1)}, u32[]{:S(2)}, u32[]{:S(2)}) %collective-permute-start.14) | collective-permute-done | bytes 8388640 | tf_op jit(solution)/shard_map/ppermute | solution.py:69
  739.3 123.1 %fusion.4 = bf16[2048,8192]{1,0:T(8,128)(2,1)} fusion(bf16[2048,8192]{1,0:T(8,128)(2,1)} %get-tuple-element.34, bf16[2048,2048]{1,0:T(8,128)(2,1)} %param.11, bf16[8192,2048]{1,0:T(8,128)(2,1)} %param.15), kind=kOutput, calls=%fused_computation.16 | convolution fusion | flops 69105352704 | bytes 109051904 | tf_op jit(solution)/shard_map/dot_general | solution.py:45
  862.6 83.4 %add_convert_fusion.1 = bf16[2048,2048]{1,0:T(8,128)(2,1)} fusion(bf16[2048,2048]{1,0:T(8,128)(2,1)} %param.11, bf16[2048,8192]{1,0:T(8,128)(2,1)} %fusion.4, bf16[2048,8192]{1,0:T(8,128)(2,1)} %param.14), kind=kOutput, calls=%fused_computation.74 | convolution fusion | flops 68732059648 | bytes 83886080 | tf_op jit(solution)/shard_map/dot_general | solution.py:45
  946.0 8.4 constant_dynamic-slice_fusion.4
  963.9 8.6 constant_dynamic-slice_fusion.1
  972.5 24.6 fusion.65
  997.0 22.6 fusion.58
  1019.7 103.5 %collective-permute-done.2 = bf16[2048,2048]{1,0:T(8,128)(2,1)} collective-permute-done((bf16[2048,2048]{1,0:T(8,128)(2,1)}, bf16[2048,2048]{1,0:T(8,128)(2,1)}, u32[]{:S(2)}, u32[]{:S(2)}) %collective-permute-start.2) | collective-permute-done | bytes 8388640 | tf_op jit(solution)/shard_map/ppermute | solution.py:69
  1123.7 24.3 fusion.63
  1148.1 25.0 fusion.108
  1173.2 24.3 fusion.109
  1197.5 24.8 fusion.110
  1222.3 41.8 %convolution_convert_fusion.3 = bf16[4096,2048]{1,0:T(8,128)(2,1)} fusion(bf16[4096,2048]{1,0:T(8,128)(2,1)} %all-gather.19.cloned.1.call-done, bf16[2048,8192]{1,0:T(8,128)(2,1)} %param.14, s32[]{:T(128)S(6)} %select_n.131), kind=kOutput, calls=%fused_computation.81 | convolution fusion | flops 34368126976 | bytes 41943044 | tf_op jit(solution)/shard_map/dot_general | solution.py:51
  1264.1 42.2 %fusion.61 = bf16[2048,4096]{0,1:T(8,128)(2,1)} fusion(bf16[4096,2048]{1,0:T(8,128)(2,1)} %all-gather.21.cloned.1.call-done, bf16[8192,2048]{1,0:T(8,128)(2,1)} %param.15, s32[]{:T(128)S(6)} %select_n.131), kind=kOutput, calls=%fused_computation.95 | convolution fusion | flops 34359738368 | bytes 41943044 | tf_op jit(solution)/shard_map/dot_general | solution.py:45
  1306.3 59.6 %add_add_fusion.1 = f32[2048,2048]{1,0:T(8,128)} fusion(f32[2048,2048]{1,0:T(8,128)} %fusion.63, f32[2048,2048]{1,0:T(8,128)} %fusion.109, bf16[4096,2048]{1,0:T(8,128)(2,1)} %all-gather.19.cloned.1.call-done, bf16[4096,2048]{1,0:T(8,128)(2,1)} %convolution_convert_fusion.3, bf16[2048,4096]{0,1:T(8,128)(2,1)} %fusion.61), kind=kOutput, calls=%fused_computation.70 | convolution fusion | flops 34552676352 | bytes 100663296 | tf_op jit(solution)/shard_map/dot_general | solution.py:48
  1374.5 47.6 %add_add_fusion = f32[2048,2048]{1,0:T(8,128)} fusion(f32[2048,2048]{1,0:T(8,128)} %fusion.58, f32[2048,2048]{1,0:T(8,128)} %fusion.110, bf16[4096,2048]{1,0:T(8,128)(2,1)} %all-gather.21.cloned.1.call-done, bf16[4096,2048]{1,0:T(8,128)(2,1)} %convolution_convert_fusion.3), kind=kOutput, calls=%fused_computation.69 | convolution fusion | flops 34452013056 | bytes 83886080 | tf_op jit(solution)/shard_map/dot_general | solution.py:48
  1431.3 42.0 %convolution_convert_fusion.2 = bf16[2048,4096]{0,1:T(8,128)(2,1)} fusion(bf16[4096,2048]{1,0:T(8,128)(2,1)} %all-gather.13.cloned.1.call-done, bf16[2048,8192]{1,0:T(8,128)(2,1)} %param.12, s32[]{:T(128)S(6)} %select_n.131), kind=kOutput, calls=%fused_computation.80 | convolution fusion | flops 34368126976 | bytes 41943044 | tf_op jit(solution)/shard_map/dot_general | solution.py:51
  1473.3 84.1 %collective-permute-done.15 = f32[4,256,2048]{2,1,0:T(8,128)} collective-permute-done((f32[4,256,2048]{2,1,0:T(8,128)}, f32[4,256,2048]{2,1,0:T(8,128)}, u32[]{:S(2)}, u32[]{:S(2)}) %collective-permute-start.15) | collective-permute-done | bytes 8388640 | tf_op jit(solution)/shard_map/ppermute | solution.py:69
  1557.4 11.9 bitcast_add_fusion
  1577.8 158.1 %collective-permute-done.21 = f32[1024,2048]{1,0:T(8,128)} collective-permute-done((f32[1024,2048]{1,0:T(8,128)}, f32[1024,2048]{1,0:T(8,128)}, u32[]{:S(2)}, u32[]{:S(2)}) %collective-permute-start.21) | collective-permute-done | bytes 8388640 | tf_op jit(solution)/shard_map/ppermute | solution.py:69
  1735.9 11.8 subtract_convert_fusion
  1747.9 50.2 %add_add_fusion.2 = f32[2048,2048]{1,0:T(8,128)} fusion(f32[2048,2048]{1,0:T(8,128)} %fusion.65, f32[2048,2048]{1,0:T(8,128)} %fusion.108, bf16[4096,2048]{1,0:T(8,128)(2,1)} %all-gather.11.cloned.1.call-done, bf16[2048,4096]{0,1:T(8,128)(2,1)} %convolution_convert_fusion.2), kind=kOutput, calls=%fused_computation.71 | convolution fusion | flops 34452013056 | bytes 83886080 | tf_op jit(solution)/shard_map/dot_general | solution.py:48
  1806.8 9.6 broadcast_select_fusion.7
  1816.4 8.5 subtract_convert_fusion.1
  1825.0 294.2 %collective-permute-done.10 = f32[1024,2048]{1,0:T(8,128)} collective-permute-done((f32[1024,2048]{1,0:T(8,128)}, f32[1024,2048]{1,0:T(8,128)}, u32[]{:S(2)}, u32[]{:S(2)}) %collective-permute-start.10) | collective-permute-done | bytes 8388640 | tf_op jit(solution)/shard_map/ppermute | solution.py:69
  2119.1 16.5 subtract_convert_fusion.2
  2135.7 123.4 %fusion.7 = bf16[2048,8192]{1,0:T(8,128)(2,1)} fusion(bf16[2048,8192]{1,0:T(8,128)(2,1)} %get-tuple-element.32, bf16[2048,2048]{1,0:T(8,128)(2,1)} %add_convert_fusion.1, bf16[8192,2048]{1,0:T(8,128)(2,1)} %param.13), kind=kOutput, calls=%fused_computation.19 | convolution fusion | flops 69105352704 | bytes 109051904 | tf_op jit(solution)/shard_map/dot_general | solution.py:45
  2259.1 8.4 constant_dynamic-slice_fusion.5
  2268.1 24.5 fusion.70
  2296.1 26.6 fusion.107
  2322.7 42.2 %fusion.68 = bf16[4096,2048]{1,0:T(8,128)(2,1)} fusion(bf16[4096,2048]{1,0:T(8,128)(2,1)} %all-gather.11.cloned.1.call-done, bf16[8192,2048]{1,0:T(8,128)(2,1)} %param.13, s32[]{:T(128)S(6)} %select_n.131), kind=kOutput, calls=%fused_computation.106 | convolution fusion | flops 34359738368 | bytes 41943044 | tf_op jit(solution)/shard_map/dot_general | solution.py:45
  2364.9 81.1 %add_add_fusion.3 = f32[2048,2048]{0,1:T(8,128)} fusion(f32[2048,2048]{0,1:T(8,128)} %fusion.70, f32[2048,2048]{0,1:T(8,128)} %fusion.107, bf16[4096,2048]{1,0:T(8,128)(2,1)} %all-gather.13.cloned.1.call-done, bf16[2048,4096]{0,1:T(8,128)(2,1)} %convolution_convert_fusion.2, bf16[4096,2048]{1,0:T(8,128)(2,1)} %fusion.68), kind=kOutput, calls=%fused_computation.72 | convolution fusion | flops 34552676352 | bytes 100663296 | tf_op jit(solution)/shard_map/dot_general | solution.py:48
  2450.3 182.2 %collective-permute-done.4 = f32[4,256,2048]{2,1,0:T(8,128)} collective-permute-done((f32[4,256,2048]{2,1,0:T(8,128)S(1)}, f32[4,256,2048]{2,1,0:T(8,128)}, u32[]{:S(2)}, u32[]{:S(2)}) %collective-permute-start.4) | collective-permute-done | bytes 8388640 | tf_op jit(solution)/shard_map/ppermute | solution.py:69
  2632.6 11.9 bitcast_add_fusion.1
  2652.1 43.1 %collective-permute-done.7 = f32[256,2048]{1,0:T(8,128)S(1)} collective-permute-done((f32[256,2048]{1,0:T(8,128)S(1)}, f32[256,2048]{1,0:T(8,128)S(1)}, u32[]{:S(2)}, u32[]{:S(2)}) %collective-permute-start.7) | collective-permute-done | bytes 2097184 | tf_op jit(solution)/shard_map/ppermute | solution.py:87
  2695.2 45.6 %collective-permute-done.5 = f32[256,2048]{1,0:T(8,128)S(1)} collective-permute-done((f32[256,2048]{1,0:T(8,128)S(1)}, f32[256,2048]{1,0:T(8,128)S(1)}, u32[]{:S(2)}, u32[]{:S(2)}) %collective-permute-start.5) | collective-permute-done | bytes 2097184 | tf_op jit(solution)/shard_map/ppermute | solution.py:87
  2747.4 8.5 subtract_convert_fusion.3
  2756.5 84.0 %add_convert_fusion = bf16[2048,2048]{1,0:T(8,128)(2,1)} fusion(bf16[2048,2048]{1,0:T(8,128)(2,1)} %add_convert_fusion.1, bf16[2048,8192]{1,0:T(8,128)(2,1)} %fusion.7, bf16[2048,8192]{1,0:T(8,128)(2,1)} %param.12), kind=kOutput, calls=%fused_computation.73 | convolution fusion | flops 68732059648 | bytes 83886080 | tf_op jit(solution)/shard_map/dot_general | solution.py:45
  2840.5 27.6 shard_map.170
  2868.1 27.3 shard_map.172
  2895.3 15.2 all-gather.15.cloned.1.call-done.src
  2910.5 29.3 shard_map.169
  2939.8 170.9 %all-gather.25.cloned.1.call-done.src = bf16[2048,8192]{1,0:T(8,128)(2,1)} async-done(((bf16[512,8192]{1,0:T(8,128)(2,1)}), bf16[2048,8192]{1,0:T(8,128)(2,1)}) %all-gather.25.cloned.1.call-update) | async-done | bytes 33554448 | tf_op jit(solution)/shard_map/all_gather | solution.py:99
  3110.6 27.2 shard_map.171
  (88 shorter events, 74.0 us)
Async XLA Ops:
  7.2 1215.1 %all-gather.19.cloned.1.call-start = ((), (), s32[]{:S(2)}) async-start(), calls=%async_computation.4 | async-start | bytes 25165824 | tf_op jit(solution)/shard_map/all_gather | solution.py:72
  193.4 184.1 %collective-permute-start.13 = (bf16[2048,2048]{1,0:T(8,128)(2,1)}, bf16[2048,2048]{1,0:T(8,128)(2,1)}, u32[]{:S(2)}, u32[]{:S(2)}) collective-permute-start(bf16[2048,2048]{1,0:T(8,128)(2,1)} %add_convert_fusion.2), channel_id=1, source_target_pairs={{0,2},{2,0},{1,3},{3,1},{4,6},{6,4},{5,7},{7,5}} | collective-permute-start | bytes 25165832 | tf_op jit(solution)/shard_map/ppermute | solution.py:69
  377.5 886.6 %all-gather.21.cloned.1.call-start = ((), (), s32[]{:S(2)}) async-start(), calls=%async_computation.5 | async-start | bytes 25165824 | tf_op jit(solution)/shard_map/all_gather | solution.py:72
  377.6 484.9 %collective-permute-start.3 = (bf16[2048,2048]{1,0:T(8,128)(2,1)}, bf16[2048,2048]{1,0:T(8,128)(2,1)}, u32[]{:S(2)}, u32[]{:S(2)}) collective-permute-start(bf16[2048,2048]{1,0:T(8,128)(2,1)} %param.10), channel_id=1, source_target_pairs={{0,2},{2,0},{1,3},{3,1},{4,6},{6,4},{5,7},{7,5}} | collective-permute-start | bytes 25165832 | tf_op jit(solution)/shard_map/ppermute | solution.py:69
  379.3 359.9 %collective-permute-start.14 = (bf16[2048,2048]{1,0:T(8,128)(2,1)}, bf16[2048,2048]{1,0:T(8,128)(2,1)}, u32[]{:S(2)}, u32[]{:S(2)}) collective-permute-start(bf16[2048,2048]{1,0:T(8,128)(2,1)} %param.11), channel_id=1, source_target_pairs={{0,2},{2,0},{1,3},{3,1},{4,6},{6,4},{5,7},{7,5}} | collective-permute-start | bytes 25165832 | tf_op jit(solution)/shard_map/ppermute | solution.py:69
  739.3 692.0 %all-gather.13.cloned.1.call-start = ((), (), s32[]{:S(2)}) async-start(), calls=%async_computation.1 | async-start | bytes 25165824 | tf_op jit(solution)/shard_map/all_gather | solution.py:72
  862.5 885.3 %all-gather.11.cloned.1.call-start = ((), (), s32[]{:S(2)}) async-start(), calls=%async_computation | async-start | bytes 25165824 | tf_op jit(solution)/shard_map/all_gather | solution.py:72
  946.0 177.2 %collective-permute-start.2 = (bf16[2048,2048]{1,0:T(8,128)(2,1)}, bf16[2048,2048]{1,0:T(8,128)(2,1)}, u32[]{:S(2)}, u32[]{:S(2)}) collective-permute-start(bf16[2048,2048]{1,0:T(8,128)(2,1)} %add_convert_fusion.1), channel_id=1, source_target_pairs={{0,2},{2,0},{1,3},{3,1},{4,6},{6,4},{5,7},{7,5}} | collective-permute-start | bytes 25165832 | tf_op jit(solution)/shard_map/ppermute | solution.py:69
  954.4 168.8 %collective-permute-start.8 = (bf16[2048,2048]{1,0:T(8,128)(2,1)}, bf16[2048,2048]{1,0:T(8,128)(2,1)}, u32[]{:S(2)}, u32[]{:S(2)}) collective-permute-start(bf16[2048,2048]{1,0:T(8,128)(2,1)} %constant_dynamic-slice_fusion.4), channel_id=1, source_target_pairs={{0,1},{1,0},{2,3},{3,2},{4,5},{5,4},{6,7},{7,6}} | collective-permute-start | bytes 25165832 | tf_op jit(solution)/shard_map/ppermute | solution.py:69
  954.4 193.7 %collective-permute-start.9 = (bf16[2048,2048]{1,0:T(8,128)(2,1)}, bf16[2048,2048]{1,0:T(8,128)(2,1)}, u32[]{:S(2)}, u32[]{:S(2)}) collective-permute-start(bf16[2048,2048]{1,0:T(8,128)(2,1)} %add_convert_fusion.1), channel_id=1, source_target_pairs={{0,1},{1,0},{2,3},{3,2},{4,5},{5,4},{6,7},{7,6}} | collective-permute-start | bytes 25165832 | tf_op jit(solution)/shard_map/ppermute | solution.py:69
  954.9 218.2 %collective-permute-start.11 = (bf16[2048,2048]{1,0:T(8,128)(2,1)}, bf16[2048,2048]{1,0:T(8,128)(2,1)}, u32[]{:S(2)}, u32[]{:S(2)}) collective-permute-start(bf16[2048,2048]{1,0:T(8,128)(2,1)} %add_convert_fusion.2), channel_id=1, source_target_pairs={{0,1},{1,0},{2,3},{3,2},{4,5},{5,4},{6,7},{7,6}} | collective-permute-start | bytes 25165832 | tf_op jit(solution)/shard_map/ppermute | solution.py:69
  963.4 209.8 %collective-permute-start.12 = (bf16[2048,2048]{1,0:T(8,128)(2,1)}, bf16[2048,2048]{1,0:T(8,128)(2,1)}, u32[]{:S(2)}, u32[]{:S(2)}) collective-permute-start(bf16[2048,2048]{1,0:T(8,128)(2,1)} %constant_dynamic-slice_fusion.2), channel_id=1, source_target_pairs={{0,1},{1,0},{2,3},{3,2},{4,5},{5,4},{6,7},{7,6}} | collective-permute-start | bytes 25165832 | tf_op jit(solution)/shard_map/ppermute | solution.py:69
  963.9 33.2 %slice-start.4 = ((s8[8388608]{0:T(1024)(128)(4,1)}), s8[4194304]{0:T(1024)(128)(4,1)S(1)}, s32[]{:S(2)}) async-start(s8[8388608]{0:T(1024)(128)(4,1)} %bitcast.122), calls=%async_computation.14 | async-start | bytes 8388608
  972.5 24.6 slice-start.5
  1123.2 74.3 %collective-permute-start.20 = (bf16[2048,2048]{1,0:T(8,128)(2,1)}, bf16[2048,2048]{1,0:T(8,128)(2,1)}, u32[]{:S(2)}, u32[]{:S(2)}) collective-permute-start(bf16[2048,2048]{1,0:T(8,128)(2,1)} %param.11), channel_id=1, source_target_pairs={{0,1},{1,0},{2,3},{3,2},{4,5},{5,4},{6,7},{7,6}} | collective-permute-start | bytes 25165832 | tf_op jit(solution)/shard_map/ppermute | solution.py:69
  1123.2 74.3 %collective-permute-start.19 = (bf16[2048,2048]{1,0:T(8,128)(2,1)}, bf16[2048,2048]{1,0:T(8,128)(2,1)}, u32[]{:S(2)}, u32[]{:S(2)}) collective-permute-start(bf16[2048,2048]{1,0:T(8,128)(2,1)} %constant_dynamic-slice_fusion.1), channel_id=1, source_target_pairs={{0,1},{1,0},{2,3},{3,2},{4,5},{5,4},{6,7},{7,6}} | collective-permute-start | bytes 25165832 | tf_op jit(solution)/shard_map/ppermute | solution.py:69
  1148.0 1120.0 %all-gather.27.cloned.1.call-start = ((), (), s32[]{:S(2)}) async-start(), calls=%async_computation.8 | async-start | bytes 12582912 | tf_op jit(solution)/shard_map/all_gather | solution.py:98
  1373.8 183.6 %collective-permute-start.15 = (f32[4,256,2048]{2,1,0:T(8,128)}, f32[4,256,2048]{2,1,0:T(8,128)}, u32[]{:S(2)}, u32[]{:S(2)}) collective-permute-start(f32[4,256,2048]{2,1,0:T(8,128)} %dynamic-slice_bitcast_fusion), channel_id=1, source_target_pairs={{0,4},{4,0},{1,5},{5,1},{2,6},{6,2},{3,7},{7,3}} | collective-permute-start | bytes 25165832 | tf_op jit(solution)/shard_map/ppermute | solution.py:69
  1430.0 305.9 %collective-permute-start.21 = (f32[1024,2048]{1,0:T(8,128)}, f32[1024,2048]{1,0:T(8,128)}, u32[]{:S(2)}, u32[]{:S(2)}) collective-permute-start(f32[1024,2048]{1,0:T(8,128)} %constant_dynamic-slice_fusion), channel_id=1, source_target_pairs={{0,4},{4,0},{1,5},{5,1},{2,6},{6,2},{3,7},{7,3}} | collective-permute-start | bytes 25165832 | tf_op jit(solution)/shard_map/ppermute | solution.py:69
  1569.3 166.6 %copy-start = (f32[1024,2048]{1,0:T(8,128)S(1)}, f32[1024,2048]{1,0:T(8,128)}, u32[]{:S(2)}) copy-start(f32[1024,2048]{1,0:T(8,128)} %param.19) | copy-start | bytes 25165828
  1575.7 231.2 %collective-permute-start.17 = (f32[256,2048]{1,0:T(8,128)}, f32[256,2048]{1,0:T(8,128)}, u32[]{:S(2)}, u32[]{:S(2)}) collective-permute-start(f32[256,2048]{1,0:T(8,128)} %get-tuple-element.27), channel_id=1, source_target_pairs={{0,1},{1,0},{2,3},{3,2},{4,5},{5,4},{6,7},{7,6}} | collective-permute-start | bytes 6291464 | tf_op jit(solution)/shard_map/ppermute | solution.py:87
  1575.7 231.2 %collective-permute-start.18 = (f32[256,2048]{1,0:T(8,128)}, f32[256,2048]{1,0:T(8,128)}, u32[]{:S(2)}, u32[]{:S(2)}) collective-permute-start(f32[256,2048]{1,0:T(8,128)} %get-tuple-element.26), channel_id=1, source_target_pairs={{0,3},{1,2},{2,1},{3,0},{4,7},{5,6},{6,5},{7,4}} | collective-permute-start | bytes 6291464 | tf_op jit(solution)/shard_map/ppermute | solution.py:87
  1576.4 230.4 %collective-permute-start.16 = (f32[256,2048]{1,0:T(8,128)}, f32[256,2048]{1,0:T(8,128)}, u32[]{:S(2)}, u32[]{:S(2)}) collective-permute-start(f32[256,2048]{1,0:T(8,128)} %get-tuple-element.25), channel_id=1, source_target_pairs={{0,2},{1,3},{2,0},{3,1},{4,6},{5,7},{6,4},{7,5}} | collective-permute-start | bytes 6291464 | tf_op jit(solution)/shard_map/ppermute | solution.py:87
  1747.8 1008.2 %all-gather.23.cloned.1.call-start = ((), (), s32[]{:S(2)}) async-start(), calls=%async_computation.6 | async-start | bytes 12582912 | tf_op jit(solution)/shard_map/all_gather | solution.py:98
  1798.0 18.4 slice-start
  1806.1 10.3 slice-start.1
  1806.1 313.1 %collective-permute-start.10 = (f32[1024,2048]{1,0:T(8,128)}, f32[1024,2048]{1,0:T(8,128)}, u32[]{:S(2)}, u32[]{:S(2)}) collective-permute-start(f32[1024,2048]{1,0:T(8,128)} %constant_dynamic-slice_fusion.3), channel_id=1, source_target_pairs={{0,4},{4,0},{1,5},{5,1},{2,6},{6,2},{3,7},{7,3}} | collective-permute-start | bytes 25165832 | tf_op jit(solution)/shard_map/ppermute | solution.py:69
  1824.9 1015.6 %all-gather.17.cloned.1.call-start = ((), (), s32[]{:S(2)}) async-start(), calls=%async_computation.3 | async-start | bytes 37748736 | tf_op jit(solution)/shard_map/all_gather | solution.py:101
  2135.7 732.4 %all-gather.29.cloned.1.call-start = ((), (), s32[]{:S(2)}) async-start(), calls=%async_computation.9 | async-start | bytes 41943040 | tf_op jit(solution)/shard_map/all_gather | solution.py:99
  2267.6 25.1 collective-permute-start
  2267.6 28.5 collective-permute-start.1
  2268.1 642.4 %all-gather.15.cloned.1.call-start = ((), (), s32[]{:S(2)}) async-start(), calls=%async_computation.2 | async-start | bytes 37748736 | tf_op jit(solution)/shard_map/all_gather | solution.py:101
  2450.3 182.3 %collective-permute-start.4 = (f32[4,256,2048]{2,1,0:T(8,128)S(1)}, f32[4,256,2048]{2,1,0:T(8,128)}, u32[]{:S(2)}, u32[]{:S(2)}) collective-permute-start(f32[4,256,2048]{2,1,0:T(8,128)S(1)} %dynamic-slice_bitcast_fusion.1), channel_id=1, source_target_pairs={{0,4},{4,0},{1,5},{5,1},{2,6},{6,2},{3,7},{7,3}} | collective-permute-start | bytes 25165832 | tf_op jit(solution)/shard_map/ppermute | solution.py:69
  2644.4 102.9 %slice-start.2 = ((s8[8388608]{0:T(1024)(128)(4,1)}), s8[4194304]{0:T(1024)(128)(4,1)S(1)}, s32[]{:S(2)}) async-start(s8[8388608]{0:T(1024)(128)(4,1)} %bitcast.120), calls=%async_computation.12 | async-start | bytes 8388608
  2647.9 4.2 collective-permute-start.6
  2647.9 47.3 %collective-permute-start.7 = (f32[256,2048]{1,0:T(8,128)S(1)}, f32[256,2048]{1,0:T(8,128)S(1)}, u32[]{:S(2)}, u32[]{:S(2)}) collective-permute-start(f32[256,2048]{1,0:T(8,128)S(1)} %get-tuple-element.29), channel_id=1, source_target_pairs={{0,3},{1,2},{2,1},{3,0},{4,7},{5,6},{6,5},{7,4}} | collective-permute-start | bytes 6291464 | tf_op jit(solution)/shard_map/ppermute | solution.py:87
  2648.9 98.5 %slice-start.3 = ((s8[8388608]{0:T(1024)(128)(4,1)}), s8[4194304]{0:T(1024)(128)(4,1)S(1)}, s32[]{:S(2)}) async-start(s8[8388608]{0:T(1024)(128)(4,1)} %bitcast.120), calls=%async_computation.13 | async-start | bytes 8388608
  2648.9 91.9 %collective-permute-start.5 = (f32[256,2048]{1,0:T(8,128)S(1)}, f32[256,2048]{1,0:T(8,128)S(1)}, u32[]{:S(2)}, u32[]{:S(2)}) collective-permute-start(f32[256,2048]{1,0:T(8,128)S(1)} %get-tuple-element.28), channel_id=1, source_target_pairs={{0,2},{1,3},{2,0},{3,1},{4,6},{5,7},{6,4},{7,5}} | collective-permute-start | bytes 6291464 | tf_op jit(solution)/shard_map/ppermute | solution.py:87
  2755.9 354.8 %all-gather.25.cloned.1.call-start = ((), (), s32[]{:S(2)}) async-start(), calls=%async_computation.7 | async-start | bytes 41943040 | tf_op jit(solution)/shard_map/all_gather | solution.py:99
Sparse Core Ops, SparseCore 0:
  377.6 28.5 all-gather.18
  739.4 28.2 all-gather.20
  862.7 27.7 all-gather.12
  1148.2 27.8 all-gather.10
  1747.9 143.3 all-gather.26
  1892.7 191.6 all-gather.22
  2135.8 157.3 all-gather.16
  2294.7 198.7 all-gather.28
  2756.0 154.4 all-gather.14
  2911.9 198.7 all-gather.24

commit v2 on v0

v2 whole, which is shorter than its diff:
```python
import functools

import jax
import jax.numpy as jnp
from jax import lax
from jax.experimental import pallas as pl
from jax.experimental.pallas import tpu as pltpu
from jax.sharding import PartitionSpec as P


LR = 0.0005
MU = 0.9
DATA = ("dx", "dy", "dz")
f32, bf = jnp.float32, jnp.bfloat16

C0, C1 = 0.7978845608028654, 0.044715


def _gelu(z):
    t = jnp.tanh(C0 * (z + C1 * (z * z * z)))
    return z * (0.5 * t + 0.5)


def _gelu_slope(z):
    z2 = z * z
    t = jnp.tanh(C0 * (z + C1 * (z2 * z)))
    return (0.5 * t + 0.5) + (1.0 - t * t) * (z * (0.5 * C0 + (1.5 * C0 * C1) * z2))


NN = (((1,), (0,)), ((), ()))
NT = (((1,), (1,)), ((), ()))
TN = (((0,), (0,)), ((), ()))


def _dot(a, b, dims):
    return lax.dot_general(a, b, dims, preferred_element_type=f32)


def _params(n):
    return pltpu.CompilerParams(dimension_semantics=("arbitrary",) * n, vmem_limit_bytes=62 * 2**20)


def _cost(m, n, k, size=2):
    return pl.CostEstimate(flops=2 * m * n * k, bytes_accessed=2 * (m * k + k * n) + size * m * n, transcendentals=0)


def _chunks(m, c):
    return [pl.ds(s, c) for s in range(0, m, c)]


def _part(src, dst, at, per):
    @pl.when(jnp.logical_and(at >= 0, at < per))
    def _():
        for r in _chunks(src.shape[0], 256):
            dst[r, :] = src[r, :]


def _zh_body(per, idx, a, w, z, h, *part):
    for r in _chunks(a.shape[0], 512):
        zb = _dot(a[r, :], w[...], NN).astype(bf)
        z[r, :] = zb
        h[r, :] = _gelu(zb.astype(f32)).astype(bf)
    if part:
        _part(h, part[0], pl.program_id(1) - per * idx[1], per)


def _dz_body(per, idx, a, w, z, o, *part):
    for r in _chunks(a.shape[0], 512):
        d = _dot(a[r, :], w[...], NT).astype(bf).astype(f32)
        o[r, :] = (_gelu_slope(z[r, :].astype(f32)) * d).astype(bf)
    if part:
        _part(o, part[0], pl.program_id(1) - per * idx[1], per)


def _expand(kind, idx, a, w, z=None):
    m, d = a.shape
    tm, tn = 2048, 512
    own = m == tm
    f = w.shape[1] if kind == "zh" else w.shape[0]
    per = f // 4 // tn
    width = f if own else f // 4
    col = (lambda i, n, s: n) if own else (lambda i, n, s: s[0] * per + n)
    if kind == "zh":
        w_spec = pl.BlockSpec((d, tn), lambda i, n, s: (0, col(i, n, s)))
    else:
        w_spec = pl.BlockSpec((tn, d), lambda i, n, s: (col(i, n, s), 0))
    tile = pl.BlockSpec((tm, tn), lambda i, n, s: (i, n))
    outs = [tile] * (2 if kind == "zh" else 1)
    shapes = [jax.ShapeDtypeStruct((m, width), bf)] * len(outs)
    if own:
        outs.append(pl.BlockSpec((tm, tn), lambda i, n, s: (0, jnp.clip(n - per * s[1], 0, per - 1))))
        shapes.append(jax.ShapeDtypeStruct((m, f // 4), bf))
    ins = [pl.BlockSpec((tm, d), lambda i, n, s: (i, 0)), w_spec] + ([] if z is None else [tile])
    return pl.pallas_call(
        functools.partial(_zh_body if kind == "zh" else _dz_body, per),
        grid_spec=pltpu.PrefetchScalarGridSpec(num_scalar_prefetch=1, grid=(m // tm, width // tn), in_specs=ins,
                                               out_specs=outs),
        out_shape=shapes, compiler_params=_params(2), cost_estimate=_cost(m, width, d, 4),
    )(idx, a, w, *(() if z is None else (z,)))


def _contract_body(dims, a, w, x, o, acc):
    k = pl.program_id(1)

    @pl.when(k == 0)
    def _():
        for r in _chunks(a.shape[0], 256):
            acc[r, :] = x[r, :].astype(f32)

    for r in _chunks(a.shape[0], 512):
        acc[r, :] += _dot(a[r, :], w[...], dims)

    @pl.when(k == pl.num_programs(1) - 1)
    def _():
        for r in _chunks(a.shape[0], 256):
            o[r, :] = acc[r, :].astype(bf)


def _contract(a, w, x, dims):
    m, f = a.shape
    d = x.shape[1]
    tn, tk = 1024, 2048
    if dims is NN:
        w_spec = pl.BlockSpec((tk, tn), lambda n, k: (k, n))
    else:
        w_spec = pl.BlockSpec((tn, tk), lambda n, k: (n, k))
    tile = pl.BlockSpec((m, tn), lambda n, k: (0, n))
    return pl.pallas_call(
        functools.partial(_contract_body, dims), grid=(d // tn, f // tk),
        in_specs=[pl.BlockSpec((m, tk), lambda n, k: (0, k)), w_spec, tile], out_specs=tile,
        out_shape=jax.ShapeDtypeStruct((m, d), bf), scratch_shapes=[pltpu.VMEM((m, tn), f32)],
        compiler_params=_params(2), cost_estimate=_cost(m, d, f),
    )(a, w, x)


def _grad_body(per, steps, idx, *refs):
    o = refs[-1]
    k = pl.program_id(0)

    @pl.when(k == 0)
    def _():
        for r in _chunks(o.shape[0], 256):
            o[r, :] = jnp.zeros((256, o.shape[1]), f32)

    start = 0
    for s, n in enumerate(steps):
        group = refs[s * (per + 1):(s + 1) * (per + 1)]

        @pl.when(jnp.logical_and(k >= start, k < start + n))
        def _(group=group):
            for t, blk in enumerate(group[:per]):
                wide = blk.shape[1]
                for c in range(0, wide, 512):
                    part = min(wide, 512)
                    o[pl.ds(t * wide + c, part), :] += _dot(blk[:, pl.ds(c, part)], group[per][...], TN)

        start += n


def _grad(idx, sources, a_cols, b_cols, tall):
    tk = 512
    wide = 1024 // tall
    steps = [a.shape[0] // tk for a, _ in sources]
    n_cols = 2048
    specs, args, start = [], [], 0
    for s, (a, b) in enumerate(sources):
        def at(k, start=start, n=steps[s]):
            return jnp.clip(k - start, 0, n - 1)

        for t in range(tall):
            specs.append(pl.BlockSpec((tk, wide), lambda k, i, at=at, s=s, t=t: (at(k), a_cols[s](i, t))))
            args.append(a)
        specs.append(pl.BlockSpec((tk, n_cols), lambda k, i, at=at, s=s: (at(k), b_cols[s](i))))
        args.append(b)
        start += steps[s]
    return pl.pallas_call(
        functools.partial(_grad_body, tall, steps),
        grid_spec=pltpu.PrefetchScalarGridSpec(num_scalar_prefetch=1, grid=(start,), in_specs=specs,
                                               out_specs=pl.BlockSpec((1024, n_cols), lambda k, i: (0, 0))),
        out_shape=jax.ShapeDtypeStruct((1024, n_cols), f32), compiler_params=_params(1),
        cost_estimate=_cost(1024, n_cols, start * tk, 4),
    )(idx, *args)


def _copy_block(src, dst):
    dst[...] = src[...]


def _move(body, grid, idx, ins, in_specs, outs, out_specs):
    size = sum(a.size * a.dtype.itemsize for a in outs)
    return pl.pallas_call(
        body, grid_spec=pltpu.PrefetchScalarGridSpec(num_scalar_prefetch=1, grid=grid, in_specs=in_specs,
                                                     out_specs=out_specs),
        out_shape=outs, compiler_params=_params(len(grid)),
        cost_estimate=pl.CostEstimate(flops=size, bytes_accessed=2 * size, transcendentals=0),
    )(idx, *ins)


def _copy(a):
    r, c = a.shape
    spec = pl.BlockSpec(((1 << 20) // c, c), lambda b: (b, 0))
    return pl.pallas_call(_copy_block, grid=(r * c >> 20,), in_specs=[spec], out_specs=spec,
                          out_shape=jax.ShapeDtypeStruct(a.shape, a.dtype), compiler_params=_params(1),
                          cost_estimate=pl.CostEstimate(flops=r * c, bytes_accessed=4 * r * c, transcendentals=0))(a)


def _deal_body(idx, *refs):
    for t in range(4):
        refs[8 + t][...] = refs[t][...] + refs[4 + t][...]


def _deal(idx, s, r):
    rows, cols = s.shape[0] // 4, s.shape[1]
    tr = 64
    per = rows // tr
    ins = [pl.BlockSpec((tr, cols), lambda b, i, t=t: ((i[0] ^ t) * per + b, 0)) for t in range(4)]
    return _move(_deal_body, (per,), idx, [s] * 4 + [r] * 4, ins * 2,
                 [jax.ShapeDtypeStruct((rows, cols), f32)] * 4, [pl.BlockSpec((tr, cols), lambda b, i: (b, 0))] * 4)


def _step(m, g, w, n, m_new, w_new):
    v = MU * m[...] + g / n
    m_new[...] = v
    w_new[...] = (w[...].astype(f32) - LR * v).astype(bf)


def _update_f_body(n, idx, m, w, s, r, m_new, w_new):
    _step(m, s[...] + r[...], w, n, m_new, w_new)


def _update_d_body(n, idx, m, w, *refs):
    for t in range(4):
        @pl.when(pl.program_id(1) == (idx[0] ^ t))
        def _(t=t):
            _step(m, refs[t][...], w, n, refs[4], refs[5])


def _update(n, idx, m, w, terms):
    rows, cols = m.shape
    outs = [jax.ShapeDtypeStruct(m.shape, f32), jax.ShapeDtypeStruct(m.shape, bf)]
    if len(terms) == 2:
        tr = 128
        per = rows // tr
        tile = pl.BlockSpec((tr, cols), lambda b, i: (b, 0))
        w_tile = pl.BlockSpec((tr, cols), lambda b, i: (i[3] * per + b, 0))
        return _move(functools.partial(_update_f_body, n), (per,), idx, [m, w, *terms],
                     [tile, w_tile, tile, tile], outs, [tile, tile])
    tr, tc = 128, cols // 4
    per = rows // tr
    tile = pl.BlockSpec((tr, tc), lambda b, c, i: (b, c))
    w_tile = pl.BlockSpec((tr, tc), lambda b, c, i: (i[3] * per + b, c))
    term = pl.BlockSpec((tr, tc), lambda b, c, i: (b, 0))
    return _move(functools.partial(_update_d_body, n), (per, 4), idx, [m, w, *terms], [tile, w_tile] + [term] * 4,
                 outs, [tile, tile])


def _join_body(idx, a, b, o):
    mine = pl.program_id(0) == idx[2]

    @pl.when(mine)
    def _():
        o[...] = a[...]

    @pl.when(jnp.logical_not(mine))
    def _():
        o[...] = b[...]


def _join(idx, a, b):
    rows, cols = a.shape
    tr = (1 << 19) // cols
    per = rows // tr
    src = pl.BlockSpec((tr, cols), lambda h, t, i: (t, 0))
    return _move(_join_body, (2, per), idx, [a, b], [src, src], [jax.ShapeDtypeStruct((2 * rows, cols), bf)],
                 [pl.BlockSpec((tr, cols), lambda h, t, i: (h * per + t, 0))])[0]


def solution(mesh):
    ndx, ndy, ndz = mesh.shape["dx"], mesh.shape["dy"], mesh.shape["dz"]
    n = ndx * ndy * ndz
    swap = [(0, 1), (1, 0)]

    def body(x, g, w1, w2, w3, w4, m1, m2, m3, m4):
        i, j, k = lax.axis_index("dx"), lax.axis_index("dy"), lax.axis_index("dz")
        q, qp = 2 * i + j, 2 * (1 - i) + j
        send_idx = jnp.stack([q, qp, 1 - k, 2 * q + k]).astype(jnp.int32)
        keep_idx = jnp.stack([q, qp, k, 2 * q + k]).astype(jnp.int32)

        def send(a, ax):
            return lax.ppermute(a, ax, swap)

        def both(a):
            return lax.all_gather(a, "dx", axis=0, tiled=True)

        def halves(sources, a_cols, b_cols, tall):
            s = _grad(send_idx, sources, a_cols, b_cols, tall)
            r = send(s, "dz")
            s = _grad(keep_idx, sources, a_cols, b_cols, tall)
            return s, r

        def grad_f(h, h_r, h_o, c, c_p, c_o):
            return halves(((h, c), (h_r, c_p), (h_o, c_o)),
                          (lambda v, t: 2 * v[0] + v[2], lambda v, t: v[2], lambda v, t: v[2]), (lambda v: 0,) * 3, 1)

        def grad_d(a, a_p, a_o, z, z_r, z_o):
            s, r = halves(((a, z), (a_p, z_r), (a_o, z_o)), (lambda v, t: 2 * t + v[2],) * 3,
                          (lambda v: v[0], lambda v: 0, lambda v: 0), 4)
            parts = list(_deal(keep_idx, s, r))
            for t in range(1, 4):
                parts[t] = lax.ppermute(parts[t], ("dy", "dx"), [(a, a ^ (0, 2, 1, 3)[t]) for a in range(4)])
            return parts

        def update(w, m, terms, l):
            m_new, w_new = _update(n, keep_idx, m, w, terms)
            if l > 2:
                r = send(w_new, "dz")
                w_new = _join(keep_idx, w_new, r)
                w_new = lax.all_gather(w_new, ("dx", "dy"), axis=0, tiled=True)
            else:
                w_new = lax.all_gather(w_new, DATA, axis=0, tiled=True)
            return _copy(w_new), m_new

        g_x, g_p = send(g, "dy"), send(g, "dx")
        x_x, x_p = send(x, "dy"), send(x, "dx")
        z1, h1, h1_s = _expand("zh", send_idx, x, w1)
        h1_r = send(h1_s, "dx")
        h2 = _contract(h1, w2, x, NN)
        h2_x, h2_p = send(h2, "dy"), send(h2, "dx")
        g_o, h2_o, x_o = both(g_x), both(h2_x), both(x_x)
        z3, h3, h3_s = _expand("zh", send_idx, h2, w3)
        h3_r = send(h3_s, "dx")
        dz3, dz3_s = _expand("dz", send_idx, g, w4, z3)
        dz3_r = send(dz3_s, "dx")
        dh2 = _contract(dz3, w3, g, NT)
        dh2_x, dh2_p = send(dh2, "dy"), send(dh2, "dx")
        dh2_o = both(dh2_x)
        z3_o, h3_o = _expand("zh", send_idx, h2_o, w3)
        s4, r4 = grad_f(h3, h3_r, h3_o, g, g_p, g_o)
        (dz3_o,) = _expand("dz", send_idx, g_o, w4, z3_o)
        s3 = grad_d(h2, h2_p, h2_o, dz3, dz3_r, dz3_o)
        dz1, dz1_s = _expand("dz", send_idx, dh2, w2, z1)
        dz1_r = send(dz1_s, "dx")
        w4n, m4n = update(w4, m4, (s4, r4), 4)
        w3n, m3n = update(w3, m3, s3, 3)
        z1_o, h1_o = _expand("zh", send_idx, x_o, w1)
        (dz1_o,) = _expand("dz", send_idx, dh2_o, w2, z1_o)
        s1 = grad_d(x, x_p, x_o, dz1, dz1_r, dz1_o)
        s2, r2 = grad_f(h1, h1_r, h1_o, dh2, dh2_p, dh2_o)
        w1n, m1n = update(w1, m1, s1, 1)
        w2n, m2n = update(w2, m2, (s2, r2), 2)
        dx = _contract(dz1, w1, dh2, NT)
        return (dx, w1n, w2n, w3n, w4n, m1n, m2n, m3n, m4n)

    row, rep = P(DATA, None), P()
    return jax.shard_map(body, mesh=mesh,
                         in_specs=(row, row, rep, rep, rep, rep, row, row, row, row),
                         out_specs=(row, rep, rep, rep, rep, row, row, row, row),
                         check_vma=False)
```

time: 4700 us -> 3050 us (0.65)
  waiting for transfers between devices: 3440 us -> 1500 us
  Pallas kernels: 0 us -> 1500 us
  matrix products: 998 us -> 0 us
  local copies, waits for them, and re-layouts: 185 us -> 0 us
  other arithmetic: 50.7 us -> 1.18 us
    reduce_scatter x12 -> x0, waiting for transfers between devices: 2220 us -> none  [reduce_scatter(): s = lax.psum_scatter(s, ax, scatter_dimension=0, tiled=True)]
    pallas_call x0 -> x31, Pallas kernels: none -> 1500 us  [the longest x8 647 us: _expand(): pl.pallas_call(functools.partial(_zh_body if kind == 'zh' else _dz_body,...]
    ppermute x0 -> x24, waiting for transfers between devices: none -> 1500 us  [the longest x18 1320 us: send(): return lax.ppermute(a, ax, swap)]
    all_gather x12 -> x8, waiting for transfers between devices: 1220 us -> 0.07 us  [the longest x4 0.06 us: both(): return lax.all_gather(a, 'dx', axis=0, tiled=True)]
    dot_general x11 -> x0, matrix products: 998 us -> none  [the longest x1 121 us: local(): dh3 = jnp.dot(g, w4.T, preferred_element_type=f32).astype(bf)]
    unnamed x10 -> x0, local copies, waits for them, and re-layouts: 175 us -> none
    convert_element_type x4 -> x0, other arithmetic: 50.7 us -> none  [update(): return (all_gather((w_loc - LR * m_new).astype(bf)), m_new)]
  transfers between devices with their start and end apart: 24 -> 32, of which waited for: 19 -> 14; matrix products, arithmetic and copies ran while one was open for 16% -> 0% of each run, Pallas kernels for 0% -> 43%
where the time goes in v2:
time: 3050 us; the launch traced here: 3030 us
  Pallas kernels  1500 us (49%)
  waiting for transfers between devices  1500 us (49%)
    ppermute x18, waiting for transfers between devices, send(): return lax.ppermute(a, ax, swap)  1320 us
    pallas_call x8, Pallas kernels, _expand(): pl.pallas_call(functools.partial(_zh_body if kind == 'zh' else _dz_body,...  647 us
    pallas_call x8, Pallas kernels, _grad(): pl.pallas_call(functools.partial(_grad_body, tall, steps), grid_spec=pltp...  397 us
    pallas_call x3, Pallas kernels, _contract(): pl.pallas_call(functools.partial(_contract_body, dims), grid=(d // tn, f...  245 us
    ppermute x6, waiting for transfers between devices, grad_d(): lax.ppermute(parts[t], ('dy', 'dx'), [(a, a ^ (0, 2, 1, 3)[t]) for a in r...  176 us
    pallas_call x4, Pallas kernels, _copy(): pl.pallas_call(_copy_block, grid=(r * c >> 20,), in_specs=[spec], out_spe...  109 us
    pallas_call x8, Pallas kernels, _move(): pl.pallas_call(body, grid_spec=pltpu.PrefetchScalarGridSpec(num_scalar_pr...  103 us
  transfers between devices with their start and end apart: 32, of which 14 were waited for; matrix products, arithmetic and copies ran while one was open for 0% of the time, Pallas kernels for 43%

profile of v2, /device:TPU:0, one launch (start us, length us, event | category | flops | bytes accessed | tf_op | source)
XLA Modules:
  0.0 3034.8 jit_solution(10396548589161054393)
XLA Ops:
  7.8 97.8 %shard_map.169 = (bf16[2048,8192]{1,0:T(8,128)(2,1)}, bf16[2048,8192]{1,0:T(8,128)(2,1)}, bf16[2048,2048]{1,0:T(8,128)(2,1)}) custom-call(s32[4]{0:T(128)} %add_add_fusion.idx, bf16[2048,2048]{1,0:T(8,128)(2,1)} %refs_3_.3, bf16[2048,8192]{1,0:T(8,128)(2,1)} %w.24), custom_call_target="tpu_custom_call" | custom-call | flops 68719476736 | bytes 109051904 | tf_op jit(solution)/shard_map/pallas_call | solution.py:94
  105.6 80.6 %shard_map.170.a.refs_0_.refs_1_.refs_2_.refs_3_ = bf16[2048,2048]{1,0:T(8,128)(2,1)} custom-call(bf16[2048,8192]{1,0:T(8,128)(2,1)} %get-tuple-element.39.a.refs_0_, bf16[8192,2048]{1,0:T(8,128)(2,1)} %w.25, bf16[2048,2048]{1,0:T(8,128)(2,1)} %refs_3_.3), custom_call_target="tpu_custom_call" | custom-call | flops 68719476736 | bytes 75497472 | tf_op jit(solution)/shard_map/pallas_call | solution.py:128
  186.2 3.3 collective-permute-start.13
  189.5 180.8 %collective-permute-done.13 = bf16[2048,2048]{1,0:T(8,128)(2,1)} collective-permute-done((bf16[2048,2048]{1,0:T(8,128)(2,1)}, bf16[2048,2048]{1,0:T(8,128)(2,1)}, u32[]{:S(2)}, u32[]{:S(2)}) %collective-permute-start.13) | collective-permute-done | bytes 8388640 | tf_op jit(solution)/shard_map/ppermute | solution.py:290
  370.4 1.8 collective-permute-start.14
  372.1 180.2 %collective-permute-done.14 = bf16[2048,2048]{1,0:T(8,128)(2,1)} collective-permute-done((bf16[2048,2048]{1,0:T(8,128)(2,1)}, bf16[2048,2048]{1,0:T(8,128)(2,1)}, u32[]{:S(2)}, u32[]{:S(2)}) %collective-permute-start.14) | collective-permute-done | bytes 8388640 | tf_op jit(solution)/shard_map/ppermute | solution.py:290
  554.1 99.9 %shard_map.171 = (bf16[2048,8192]{1,0:T(8,128)(2,1)}, bf16[2048,8192]{1,0:T(8,128)(2,1)}, bf16[2048,2048]{1,0:T(8,128)(2,1)}) custom-call(s32[4]{0:T(128)} %add_add_fusion.idx, bf16[2048,2048]{1,0:T(8,128)(2,1)} %shard_map.170.a.refs_0_.refs_1_.refs_2_.refs_3_, bf16[2048,8192]{1,0:T(8,128)(2,1)} %w.28), custom_call_target="tpu_custom_call" | custom-call | flops 68719476736 | bytes 109051904 | tf_op jit(solution)/shard_map/pallas_call | solution.py:94
  653.9 79.7 %collective-permute-done.2 = bf16[2048,2048]{1,0:T(8,128)(2,1)} collective-permute-done((bf16[2048,2048]{1,0:T(8,128)(2,1)}, bf16[2048,2048]{1,0:T(8,128)(2,1)}, u32[]{:S(2)}, u32[]{:S(2)}) %collective-permute-start.2) | collective-permute-done | bytes 8388640 | tf_op jit(solution)/shard_map/ppermute | solution.py:290
  733.7 111.8 %shard_map.172 = (bf16[2048,8192]{1,0:T(8,128)(2,1)}, bf16[2048,2048]{1,0:T(8,128)(2,1)}) custom-call(s32[4]{0:T(128)} %add_add_fusion.idx, bf16[2048,2048]{1,0:T(8,128)(2,1)} %refs_1_.7, bf16[8192,2048]{1,0:T(8,128)(2,1)} %w.29, bf16[2048,8192]{1,0:T(8,128)(2,1)} %get-tuple-element.40.z), custom_call_target="tpu_custom_call" | custom-call | flops 68719476736 | bytes 109051904 | tf_op jit(solution)/shard_map/pallas_call | solution.py:94
  845.6 81.2 %shard_map.173.a.x.refs_1_ = bf16[2048,2048]{1,0:T(8,128)(2,1)} custom-call(bf16[2048,8192]{1,0:T(8,128)(2,1)} %get-tuple-element.41.a.refs_4_, bf16[2048,8192]{1,0:T(8,128)(2,1)} %w.28, bf16[2048,2048]{1,0:T(8,128)(2,1)} %refs_1_.7), custom_call_target="tpu_custom_call" | custom-call | flops 68719476736 | bytes 75497472 | tf_op jit(solution)/shard_map/pallas_call | solution.py:128
  927.9 177.8 %collective-permute-done.3 = bf16[2048,2048]{1,0:T(8,128)(2,1)} collective-permute-done((bf16[2048,2048]{1,0:T(8,128)(2,1)}, bf16[2048,2048]{1,0:T(8,128)(2,1)}, u32[]{:S(2)}, u32[]{:S(2)}) %collective-permute-start.3) | collective-permute-done | bytes 8388640 | tf_op jit(solution)/shard_map/ppermute | solution.py:290
  1105.8 52.9 %shard_map.187 = (bf16[4096,2048]{1,0:T(8,128)(2,1)}, bf16[4096,2048]{1,0:T(8,128)(2,1)}) custom-call(s32[4]{0:T(128)} %add_add_fusion.idx, bf16[4096,2048]{1,0:T(8,128)(2,1)} %all-gather.17.cloned.1.call-done.a.refs_10_.refs_11_.refs_12_.refs_13_, bf16[2048,8192]{1,0:T(8,128)(2,1)} %w.28), custom_call_target="tpu_custom_call" | custom-call | flops 34359738368 | bytes 58720256 | tf_op jit(solution)/shard_map/pallas_call | solution.py:94
  1158.8 48.1 %shard_map.196 = f32[1024,2048]{1,0:T(8,128)} custom-call(s32[4]{0:T(128)} %add_add_fusion.idx, bf16[2048,8192]{1,0:T(8,128)(2,1)} %get-tuple-element.61.refs_0_, bf16[2048,2048]{1,0:T(8,128)(2,1)} %refs_1_.7, bf16[2048,2048]{1,0:T(8,128)(2,1)} %collective-permute-done.20.refs_2_, bf16[2048,2048]{1,0:T(8,128)(2,1)} %collective-permute-done.21.refs_3_, ...), custom_call_target="tpu_custom_call" | custom-call | flops 34359738368 | bytes 58720256 | tf_op jit(solution)/shard_map/pallas_call | solution.py:176
  1207.6 48.6 %shard_map.195.s = f32[1024,2048]{1,0:T(8,128)} custom-call(s32[4]{0:T(128)} %add_add_fusion.1.idx, bf16[2048,8192]{1,0:T(8,128)(2,1)} %get-tuple-element.61.refs_0_, bf16[2048,2048]{1,0:T(8,128)(2,1)} %refs_1_.7, bf16[2048,2048]{1,0:T(8,128)(2,1)} %collective-permute-done.20.refs_2_, bf16[2048,2048]{1,0:T(8,128)(2,1)} %collective-permute-done.21.refs_3_, ...), custom_call_target="tpu_custom_call" | custom-call | flops 34359738368 | bytes 58720256 | tf_op jit(solution)/shard_map/pallas_call | solution.py:176
  1256.2 128.8 %collective-permute-done.22.r = f32[1024,2048]{1,0:T(8,128)} collective-permute-done((f32[1024,2048]{1,0:T(8,128)}, f32[1024,2048]{1,0:T(8,128)}, u32[]{:S(2)}, u32[]{:S(2)}) %collective-permute-start.22) | collective-permute-done | bytes 8388640 | tf_op jit(solution)/shard_map/ppermute | solution.py:290
  1385.0 15.6 shard_map.197
  1402.3 87.2 %collective-permute-done.23.b = bf16[1024,2048]{1,0:T(8,128)(2,1)} collective-permute-done((bf16[1024,2048]{1,0:T(8,128)(2,1)}, bf16[1024,2048]{1,0:T(8,128)(2,1)}, u32[]{:S(2)}, u32[]{:S(2)}) %collective-permute-start.23) | collective-permute-done | bytes 4194336 | tf_op jit(solution)/shard_map/ppermute | solution.py:290
  1489.5 11.3 shard_map.198
  1501.5 60.1 %shard_map.188.refs_14_ = bf16[4096,2048]{1,0:T(8,128)(2,1)} custom-call(s32[4]{0:T(128)} %add_add_fusion.idx, bf16[4096,2048]{1,0:T(8,128)(2,1)} %all-gather.19.cloned.1.call-done.a.refs_5_, bf16[8192,2048]{1,0:T(8,128)(2,1)} %w.29, bf16[4096,2048]{1,0:T(8,128)(2,1)} %get-tuple-element.55.z), custom_call_target="tpu_custom_call" | custom-call | flops 34359738368 | bytes 58720256 | tf_op jit(solution)/shard_map/pallas_call | solution.py:94
  1561.5 51.0 %shard_map.190 = f32[1024,2048]{1,0:T(8,128)} custom-call(s32[4]{0:T(128)} %add_add_fusion.idx, bf16[2048,2048]{1,0:T(8,128)(2,1)} %shard_map.170.a.refs_0_.refs_1_.refs_2_.refs_3_, bf16[2048,2048]{1,0:T(8,128)(2,1)} %shard_map.170.a.refs_0_.refs_1_.refs_2_.refs_3_, bf16[2048,2048]{1,0:T(8,128)(2,1)} %shard_map.170.a.refs_0_.refs_1_.refs_2_.refs_3_, ...), custom_call_target="tpu_custom_call" | custom-call | flops 34359738368 | bytes 58720256 | tf_op jit(solution)/shard_map/pallas_call | solution.py:176
  1614.1 50.8 %shard_map.189.refs_0_.refs_1_.refs_2_.refs_3_ = f32[1024,2048]{1,0:T(8,128)} custom-call(s32[4]{0:T(128)} %add_add_fusion.1.idx, bf16[2048,2048]{1,0:T(8,128)(2,1)} %shard_map.170.a.refs_0_.refs_1_.refs_2_.refs_3_, bf16[2048,2048]{1,0:T(8,128)(2,1)} %shard_map.170.a.refs_0_.refs_1_.refs_2_.refs_3_, ...), custom_call_target="tpu_custom_call" | custom-call | flops 34359738368 | bytes 58720256 | tf_op jit(solution)/shard_map/pallas_call | solution.py:176
  1664.9 130.0 %collective-permute-done.15.refs_4_.refs_5_.refs_6_.refs_7_ = f32[1024,2048]{1,0:T(8,128)} collective-permute-done((f32[1024,2048]{1,0:T(8,128)}, f32[1024,2048]{1,0:T(8,128)}, u32[]{:S(2)}, u32[]{:S(2)}) %collective-permute-start.15) | collective-permute-done | bytes 8388640 | tf_op jit(solution)/shard_map/ppermute | solution.py:290
  1794.9 9.7 shard_map.191
  1806.7 46.7 %collective-permute-done.16.refs_1_ = f32[256,2048]{1,0:T(8,128)} collective-permute-done((f32[256,2048]{1,0:T(8,128)}, f32[256,2048]{1,0:T(8,128)}, u32[]{:S(2)}, u32[]{:S(2)}) %collective-permute-start.16) | collective-permute-done | bytes 2097184 | tf_op jit(solution)/shard_map/ppermute | solution.py:310
  1853.4 41.8 %collective-permute-done.18.refs_3_ = f32[256,2048]{1,0:T(8,128)} collective-permute-done((f32[256,2048]{1,0:T(8,128)}, f32[256,2048]{1,0:T(8,128)}, u32[]{:S(2)}, u32[]{:S(2)}) %collective-permute-start.18) | collective-permute-done | bytes 2097184 | tf_op jit(solution)/shard_map/ppermute | solution.py:310
  1895.2 15.1 shard_map.192
  1911.3 92.8 %collective-permute-done.19.b = bf16[256,8192]{1,0:T(8,128)(2,1)} collective-permute-done((bf16[256,8192]{1,0:T(8,128)(2,1)}, bf16[256,8192]{1,0:T(8,128)(2,1)}, u32[]{:S(2)}, u32[]{:S(2)}) %collective-permute-start.19) | collective-permute-done | bytes 4194336 | tf_op jit(solution)/shard_map/ppermute | solution.py:290
  2004.1 11.3 shard_map.193
  2016.1 54.0 %shard_map.176 = (bf16[4096,2048]{1,0:T(8,128)(2,1)}, bf16[4096,2048]{1,0:T(8,128)(2,1)}) custom-call(s32[4]{0:T(128)} %add_add_fusion.idx, bf16[4096,2048]{1,0:T(8,128)(2,1)} %all-gather.9.cloned.1.call-done.a.refs_10_.refs_11_.refs_12_.refs_13_, bf16[2048,8192]{1,0:T(8,128)(2,1)} %w.24), custom_call_target="tpu_custom_call" | custom-call | flops 34359738368 | bytes 58720256 | tf_op jit(solution)/shard_map/pallas_call | solution.py:94
  2070.1 48.1 %shard_map.184 = f32[1024,2048]{1,0:T(8,128)} custom-call(s32[4]{0:T(128)} %add_add_fusion.idx, bf16[2048,8192]{1,0:T(8,128)(2,1)} %get-tuple-element.39.a.refs_0_, bf16[2048,2048]{1,0:T(8,128)(2,1)} %shard_map.173.a.x.refs_1_, bf16[2048,2048]{1,0:T(8,128)(2,1)} %collective-permute-done.8.refs_2_, bf16[2048,2048]{1,0:T(8,128)(2,1)} %collective-permute-done.9.refs_3_, ...), custom_call_target="tpu_custom_call" | custom-call | flops 34359738368 | bytes 58720256 | tf_op jit(solution)/shard_map/pallas_call | solution.py:176
  2118.2 48.3 %shard_map.183.s = f32[1024,2048]{1,0:T(8,128)} custom-call(s32[4]{0:T(128)} %add_add_fusion.1.idx, bf16[2048,8192]{1,0:T(8,128)(2,1)} %get-tuple-element.39.a.refs_0_, bf16[2048,2048]{1,0:T(8,128)(2,1)} %shard_map.173.a.x.refs_1_, bf16[2048,2048]{1,0:T(8,128)(2,1)} %collective-permute-done.8.refs_2_, bf16[2048,2048]{1,0:T(8,128)(2,1)} %collective-permute-done.9.refs_3_, ...), custom_call_target="tpu_custom_call" | custom-call | flops 34359738368 | bytes 58720256 | tf_op jit(solution)/shard_map/pallas_call | solution.py:176
  2166.5 134.3 %collective-permute-done.10.r = f32[1024,2048]{1,0:T(8,128)} collective-permute-done((f32[1024,2048]{1,0:T(8,128)}, f32[1024,2048]{1,0:T(8,128)}, u32[]{:S(2)}, u32[]{:S(2)}) %collective-permute-start.10) | collective-permute-done | bytes 8388640 | tf_op jit(solution)/shard_map/ppermute | solution.py:290
  2300.7 15.6 shard_map.185
  2316.4 112.6 %shard_map.174 = (bf16[2048,8192]{1,0:T(8,128)(2,1)}, bf16[2048,2048]{1,0:T(8,128)(2,1)}) custom-call(s32[4]{0:T(128)} %add_add_fusion.idx, bf16[2048,2048]{1,0:T(8,128)(2,1)} %shard_map.173.a.x.refs_1_, bf16[8192,2048]{1,0:T(8,128)(2,1)} %w.25, bf16[2048,8192]{1,0:T(8,128)(2,1)} %get-tuple-element.42.z), custom_call_target="tpu_custom_call" | custom-call | flops 68719476736 | bytes 109051904 | tf_op jit(solution)/shard_map/pallas_call | solution.py:94
  2429.5 57.9 %shard_map.177.refs_14_ = bf16[4096,2048]{1,0:T(8,128)(2,1)} custom-call(s32[4]{0:T(128)} %add_add_fusion.idx, bf16[4096,2048]{1,0:T(8,128)(2,1)} %all-gather.11.cloned.1.call-done.a.refs_5_, bf16[8192,2048]{1,0:T(8,128)(2,1)} %w.25, bf16[4096,2048]{1,0:T(8,128)(2,1)} %get-tuple-element.45.z), custom_call_target="tpu_custom_call" | custom-call | flops 34359738368 | bytes 58720256 | tf_op jit(solution)/shard_map/pallas_call | solution.py:94
  2487.4 50.9 %shard_map.179 = f32[1024,2048]{1,0:T(8,128)} custom-call(s32[4]{0:T(128)} %add_add_fusion.idx, bf16[2048,2048]{1,0:T(8,128)(2,1)} %refs_3_.3, bf16[2048,2048]{1,0:T(8,128)(2,1)} %refs_3_.3, bf16[2048,2048]{1,0:T(8,128)(2,1)} %refs_3_.3, bf16[2048,2048]{1,0:T(8,128)(2,1)} %refs_3_.3, bf16[2048,8192]{1,0:T(8,128)(2,1)} %get-tuple-element.43.a.refs_4_, ...), custom_call_target="tpu_custom_call" | custom-call | flops 34359738368 | bytes 58720256 | tf_op jit(solution)/shard_map/pallas_call | solution.py:176
  2538.4 51.1 %shard_map.178.refs_0_.refs_1_.refs_2_.refs_3_ = f32[1024,2048]{1,0:T(8,128)} custom-call(s32[4]{0:T(128)} %add_add_fusion.1.idx, bf16[2048,2048]{1,0:T(8,128)(2,1)} %refs_3_.3, bf16[2048,2048]{1,0:T(8,128)(2,1)} %refs_3_.3, bf16[2048,2048]{1,0:T(8,128)(2,1)} %refs_3_.3, bf16[2048,2048]{1,0:T(8,128)(2,1)} %refs_3_.3, ...), custom_call_target="tpu_custom_call" | custom-call | flops 34359738368 | bytes 58720256 | tf_op jit(solution)/shard_map/pallas_call | solution.py:176
  2589.5 131.5 %collective-permute-done.4.refs_4_.refs_5_.refs_6_.refs_7_ = f32[1024,2048]{1,0:T(8,128)} collective-permute-done((f32[1024,2048]{1,0:T(8,128)}, f32[1024,2048]{1,0:T(8,128)}, u32[]{:S(2)}, u32[]{:S(2)}) %collective-permute-start.4) | collective-permute-done | bytes 8388640 | tf_op jit(solution)/shard_map/ppermute | solution.py:290
  2721.0 9.7 shard_map.180
  2730.7 2.1 collective-permute-start.7
  2732.8 46.7 %collective-permute-done.5.refs_1_ = f32[256,2048]{1,0:T(8,128)} collective-permute-done((f32[256,2048]{1,0:T(8,128)}, f32[256,2048]{1,0:T(8,128)}, u32[]{:S(2)}, u32[]{:S(2)}) %collective-permute-start.5) | collective-permute-done | bytes 2097184 | tf_op jit(solution)/shard_map/ppermute | solution.py:310
  2779.5 41.3 %collective-permute-done.7.refs_3_ = f32[256,2048]{1,0:T(8,128)} collective-permute-done((f32[256,2048]{1,0:T(8,128)}, f32[256,2048]{1,0:T(8,128)}, u32[]{:S(2)}, u32[]{:S(2)}) %collective-permute-start.7) | collective-permute-done | bytes 2097184 | tf_op jit(solution)/shard_map/ppermute | solution.py:310
  2820.8 15.1 shard_map.181
  2836.0 82.8 %shard_map.175 = bf16[2048,2048]{1,0:T(8,128)(2,1)} custom-call(bf16[2048,8192]{1,0:T(8,128)(2,1)} %get-tuple-element.43.a.refs_4_, bf16[2048,8192]{1,0:T(8,128)(2,1)} %w.24, bf16[2048,2048]{1,0:T(8,128)(2,1)} %shard_map.173.a.x.refs_1_), custom_call_target="tpu_custom_call" | custom-call | flops 68719476736 | bytes 75497472 | tf_op jit(solution)/shard_map/pallas_call | solution.py:128
  2918.7 27.3 shard_map.199
  2946.0 27.3 shard_map.194
  2973.3 27.3 shard_map.186
  3000.6 27.2 shard_map.182
  (57 shorter events, 12.6 us)
Async XLA Ops:
  7.2 1098.6 %all-gather.17.cloned.1.call-start = ((), (), s32[]{:S(2)}) async-start(), calls=%async_computation.4 | async-start | bytes 25165824 | tf_op jit(solution)/shard_map/all_gather | solution.py:293
  186.2 184.1 %collective-permute-start.13 = (bf16[2048,2048]{1,0:T(8,128)(2,1)}, bf16[2048,2048]{1,0:T(8,128)(2,1)}, u32[]{:S(2)}, u32[]{:S(2)}) collective-permute-start(bf16[2048,2048]{1,0:T(8,128)(2,1)} %shard_map.170.a.refs_0_.refs_1_.refs_2_.refs_3_), channel_id=1, source_target_pairs={{0,2},{2,0},{1,3},{3,1},{4,6},{6,4},{5,7},{7,5}} | collective-permute-start | bytes 25165832 | tf_op jit(solution)/shard_map/ppermute | solution.py:290
  370.3 788.4 %all-gather.19.cloned.1.call-start = ((), (), s32[]{:S(2)}) async-start(), calls=%async_computation.5 | async-start | bytes 25165824 | tf_op jit(solution)/shard_map/all_gather | solution.py:293
  370.4 182.0 %collective-permute-start.14 = (bf16[2048,2048]{1,0:T(8,128)(2,1)}, bf16[2048,2048]{1,0:T(8,128)(2,1)}, u32[]{:S(2)}, u32[]{:S(2)}) collective-permute-start(bf16[2048,2048]{1,0:T(8,128)(2,1)} %refs_1_.7), channel_id=1, source_target_pairs={{0,2},{2,0},{1,3},{3,1},{4,6},{6,4},{5,7},{7,5}} | collective-permute-start | bytes 25165832 | tf_op jit(solution)/shard_map/ppermute | solution.py:290
  552.3 1463.7 %all-gather.9.cloned.1.call-start = ((), (), s32[]{:S(2)}) async-start(), calls=%async_computation | async-start | bytes 25165824 | tf_op jit(solution)/shard_map/all_gather | solution.py:293
  552.6 181.1 %collective-permute-start.2 = (bf16[2048,2048]{1,0:T(8,128)(2,1)}, bf16[2048,2048]{1,0:T(8,128)(2,1)}, u32[]{:S(2)}, u32[]{:S(2)}) collective-permute-start(bf16[2048,2048]{1,0:T(8,128)(2,1)} %refs_3_.3), channel_id=1, source_target_pairs={{0,2},{2,0},{1,3},{3,1},{4,6},{6,4},{5,7},{7,5}} | collective-permute-start | bytes 25165832 | tf_op jit(solution)/shard_map/ppermute | solution.py:290
  733.7 1336.4 %all-gather.11.cloned.1.call-start = ((), (), s32[]{:S(2)}) async-start(), calls=%async_computation.1 | async-start | bytes 25165824 | tf_op jit(solution)/shard_map/all_gather | solution.py:293
  926.7 179.0 %collective-permute-start.3 = (bf16[2048,2048]{1,0:T(8,128)(2,1)}, bf16[2048,2048]{1,0:T(8,128)(2,1)}, u32[]{:S(2)}, u32[]{:S(2)}) collective-permute-start(bf16[2048,2048]{1,0:T(8,128)(2,1)} %shard_map.173.a.x.refs_1_), channel_id=1, source_target_pairs={{0,2},{2,0},{1,3},{3,1},{4,6},{6,4},{5,7},{7,5}} | collective-permute-start | bytes 25165832 | tf_op jit(solution)/shard_map/ppermute | solution.py:290
  927.4 231.4 %collective-permute-start.20 = (bf16[2048,2048]{1,0:T(8,128)(2,1)}, bf16[2048,2048]{1,0:T(8,128)(2,1)}, u32[]{:S(2)}, u32[]{:S(2)}) collective-permute-start(bf16[2048,2048]{1,0:T(8,128)(2,1)} %get-tuple-element.62), channel_id=1, source_target_pairs={{0,1},{1,0},{2,3},{3,2},{4,5},{5,4},{6,7},{7,6}} | collective-permute-start | bytes 25165832 | tf_op jit(solution)/shard_map/ppermute | solution.py:290
  927.4 231.4 %collective-permute-start.21 = (bf16[2048,2048]{1,0:T(8,128)(2,1)}, bf16[2048,2048]{1,0:T(8,128)(2,1)}, u32[]{:S(2)}, u32[]{:S(2)}) collective-permute-start(bf16[2048,2048]{1,0:T(8,128)(2,1)} %refs_1_.7), channel_id=1, source_target_pairs={{0,1},{1,0},{2,3},{3,2},{4,5},{5,4},{6,7},{7,6}} | collective-permute-start | bytes 25165832 | tf_op jit(solution)/shard_map/ppermute | solution.py:290
  1105.7 1813.0 %all-gather.23.cloned.1.call-start = ((), (), s32[]{:S(2)}) async-start(), calls=%async_computation.7 | async-start | bytes 41943040 | tf_op jit(solution)/shard_map/all_gather | solution.py:318
  1206.9 178.1 %collective-permute-start.22 = (f32[1024,2048]{1,0:T(8,128)}, f32[1024,2048]{1,0:T(8,128)}, u32[]{:S(2)}, u32[]{:S(2)}) collective-permute-start(f32[1024,2048]{1,0:T(8,128)} %shard_map.196), channel_id=1, source_target_pairs={{0,4},{4,0},{1,5},{5,1},{2,6},{6,2},{3,7},{7,3}} | collective-permute-start | bytes 25165832 | tf_op jit(solution)/shard_map/ppermute | solution.py:290
  1400.5 89.0 %collective-permute-start.23 = (bf16[1024,2048]{1,0:T(8,128)(2,1)}, bf16[1024,2048]{1,0:T(8,128)(2,1)}, u32[]{:S(2)}, u32[]{:S(2)}) collective-permute-start(bf16[1024,2048]{1,0:T(8,128)(2,1)} %get-tuple-element.64.a), channel_id=1, source_target_pairs={{0,4},{4,0},{1,5},{5,1},{2,6},{6,2},{3,7},{7,3}} | collective-permute-start | bytes 12582920 | tf_op jit(solution)/shard_map/ppermute | solution.py:290
  1500.9 1445.1 %all-gather.21.cloned.1.call-start = ((), (), s32[]{:S(2)}) async-start(), calls=%async_computation.6 | async-start | bytes 41943040 | tf_op jit(solution)/shard_map/all_gather | solution.py:318
  1500.9 60.6 %collective-permute-start.12 = (bf16[2048,2048]{1,0:T(8,128)(2,1)}, bf16[2048,2048]{1,0:T(8,128)(2,1)}, u32[]{:S(2)}, u32[]{:S(2)}) collective-permute-start(bf16[2048,2048]{1,0:T(8,128)(2,1)} %get-tuple-element.54), channel_id=1, source_target_pairs={{0,1},{1,0},{2,3},{3,2},{4,5},{5,4},{6,7},{7,6}} | collective-permute-start | bytes 25165832 | tf_op jit(solution)/shard_map/ppermute | solution.py:290
  1501.0 60.6 %collective-permute-start.11 = (bf16[2048,2048]{1,0:T(8,128)(2,1)}, bf16[2048,2048]{1,0:T(8,128)(2,1)}, u32[]{:S(2)}, u32[]{:S(2)}) collective-permute-start(bf16[2048,2048]{1,0:T(8,128)(2,1)} %shard_map.170.a.refs_0_.refs_1_.refs_2_.refs_3_), channel_id=1, source_target_pairs={{0,1},{1,0},{2,3},{3,2},{4,5},{5,4},{6,7},{7,6}} | collective-permute-start | bytes 25165832 | tf_op jit(solution)/shard_map/ppermute | solution.py:290
  1612.5 182.4 %collective-permute-start.15 = (f32[1024,2048]{1,0:T(8,128)}, f32[1024,2048]{1,0:T(8,128)}, u32[]{:S(2)}, u32[]{:S(2)}) collective-permute-start(f32[1024,2048]{1,0:T(8,128)} %shard_map.190), channel_id=1, source_target_pairs={{0,4},{4,0},{1,5},{5,1},{2,6},{6,2},{3,7},{7,3}} | collective-permute-start | bytes 25165832 | tf_op jit(solution)/shard_map/ppermute | solution.py:290
  1804.6 48.8 %collective-permute-start.16 = (f32[256,2048]{1,0:T(8,128)}, f32[256,2048]{1,0:T(8,128)}, u32[]{:S(2)}, u32[]{:S(2)}) collective-permute-start(f32[256,2048]{1,0:T(8,128)} %get-tuple-element.57), channel_id=1, source_target_pairs={{0,2},{1,3},{2,0},{3,1},{4,6},{5,7},{6,4},{7,5}} | collective-permute-start | bytes 6291464 | tf_op jit(solution)/shard_map/ppermute | solution.py:310
  1805.9 47.5 %collective-permute-start.17 = (f32[256,2048]{1,0:T(8,128)}, f32[256,2048]{1,0:T(8,128)}, u32[]{:S(2)}, u32[]{:S(2)}) collective-permute-start(f32[256,2048]{1,0:T(8,128)} %get-tuple-element.58), channel_id=1, source_target_pairs={{0,1},{1,0},{2,3},{3,2},{4,5},{5,4},{6,7},{7,6}} | collective-permute-start | bytes 6291464 | tf_op jit(solution)/shard_map/ppermute | solution.py:310
  1805.9 89.3 %collective-permute-start.18 = (f32[256,2048]{1,0:T(8,128)}, f32[256,2048]{1,0:T(8,128)}, u32[]{:S(2)}, u32[]{:S(2)}) collective-permute-start(f32[256,2048]{1,0:T(8,128)} %get-tuple-element.59), channel_id=1, source_target_pairs={{0,3},{1,2},{2,1},{3,0},{4,7},{5,6},{6,5},{7,4}} | collective-permute-start | bytes 6291464 | tf_op jit(solution)/shard_map/ppermute | solution.py:310
  1910.4 93.7 %collective-permute-start.19 = (bf16[256,8192]{1,0:T(8,128)(2,1)}, bf16[256,8192]{1,0:T(8,128)(2,1)}, u32[]{:S(2)}, u32[]{:S(2)}) collective-permute-start(bf16[256,8192]{1,0:T(8,128)(2,1)} %get-tuple-element.60.a), channel_id=1, source_target_pairs={{0,4},{4,0},{1,5},{5,1},{2,6},{6,2},{3,7},{7,3}} | collective-permute-start | bytes 12582920 | tf_op jit(solution)/shard_map/ppermute | solution.py:290
  2015.5 957.8 %all-gather.15.cloned.1.call-start = ((), (), s32[]{:S(2)}) async-start(), calls=%async_computation.3 | async-start | bytes 37748736 | tf_op jit(solution)/shard_map/all_gather | solution.py:320
  2015.5 54.5 %collective-permute-start.9 = (bf16[2048,2048]{1,0:T(8,128)(2,1)}, bf16[2048,2048]{1,0:T(8,128)(2,1)}, u32[]{:S(2)}, u32[]{:S(2)}) collective-permute-start(bf16[2048,2048]{1,0:T(8,128)(2,1)} %shard_map.173.a.x.refs_1_), channel_id=1, source_target_pairs={{0,1},{1,0},{2,3},{3,2},{4,5},{5,4},{6,7},{7,6}} | collective-permute-start | bytes 25165832 | tf_op jit(solution)/shard_map/ppermute | solution.py:290
  2015.7 54.4 %collective-permute-start.8 = (bf16[2048,2048]{1,0:T(8,128)(2,1)}, bf16[2048,2048]{1,0:T(8,128)(2,1)}, u32[]{:S(2)}, u32[]{:S(2)}) collective-permute-start(bf16[2048,2048]{1,0:T(8,128)(2,1)} %get-tuple-element.51), channel_id=1, source_target_pairs={{0,1},{1,0},{2,3},{3,2},{4,5},{5,4},{6,7},{7,6}} | collective-permute-start | bytes 25165832 | tf_op jit(solution)/shard_map/ppermute | solution.py:290
  2118.2 182.6 %collective-permute-start.10 = (f32[1024,2048]{1,0:T(8,128)}, f32[1024,2048]{1,0:T(8,128)}, u32[]{:S(2)}, u32[]{:S(2)}) collective-permute-start(f32[1024,2048]{1,0:T(8,128)} %shard_map.184), channel_id=1, source_target_pairs={{0,4},{4,0},{1,5},{5,1},{2,6},{6,2},{3,7},{7,3}} | collective-permute-start | bytes 25165832 | tf_op jit(solution)/shard_map/ppermute | solution.py:290
  2316.3 684.2 %all-gather.13.cloned.1.call-start = ((), (), s32[]{:S(2)}) async-start(), calls=%async_computation.2 | async-start | bytes 37748736 | tf_op jit(solution)/shard_map/all_gather | solution.py:320
  2429.0 58.4 %collective-permute-start.1 = (bf16[2048,2048]{1,0:T(8,128)(2,1)}, bf16[2048,2048]{1,0:T(8,128)(2,1)}, u32[]{:S(2)}, u32[]{:S(2)}) collective-permute-start(bf16[2048,2048]{1,0:T(8,128)(2,1)} %get-tuple-element.44), channel_id=1, source_target_pairs={{0,1},{1,0},{2,3},{3,2},{4,5},{5,4},{6,7},{7,6}} | collective-permute-start | bytes 25165832 | tf_op jit(solution)/shard_map/ppermute | solution.py:290
  2429.0 58.4 %collective-permute-start = (bf16[2048,2048]{1,0:T(8,128)(2,1)}, bf16[2048,2048]{1,0:T(8,128)(2,1)}, u32[]{:S(2)}, u32[]{:S(2)}) collective-permute-start(bf16[2048,2048]{1,0:T(8,128)(2,1)} %refs_3_.3), channel_id=1, source_target_pairs={{0,1},{1,0},{2,3},{3,2},{4,5},{5,4},{6,7},{7,6}} | collective-permute-start | bytes 25165832 | tf_op jit(solution)/shard_map/ppermute | solution.py:290
  2538.3 182.7 %collective-permute-start.4 = (f32[1024,2048]{1,0:T(8,128)}, f32[1024,2048]{1,0:T(8,128)}, u32[]{:S(2)}, u32[]{:S(2)}) collective-permute-start(f32[1024,2048]{1,0:T(8,128)} %shard_map.179), channel_id=1, source_target_pairs={{0,4},{4,0},{1,5},{5,1},{2,6},{6,2},{3,7},{7,3}} | collective-permute-start | bytes 25165832 | tf_op jit(solution)/shard_map/ppermute | solution.py:290
  2730.7 48.8 %collective-permute-start.5 = (f32[256,2048]{1,0:T(8,128)}, f32[256,2048]{1,0:T(8,128)}, u32[]{:S(2)}, u32[]{:S(2)}) collective-permute-start(f32[256,2048]{1,0:T(8,128)} %get-tuple-element.47), channel_id=1, source_target_pairs={{0,2},{1,3},{2,0},{3,1},{4,6},{5,7},{6,4},{7,5}} | collective-permute-start | bytes 6291464 | tf_op jit(solution)/shard_map/ppermute | solution.py:310
  2730.7 48.8 %collective-permute-start.6 = (f32[256,2048]{1,0:T(8,128)}, f32[256,2048]{1,0:T(8,128)}, u32[]{:S(2)}, u32[]{:S(2)}) collective-permute-start(f32[256,2048]{1,0:T(8,128)} %get-tuple-element.48), channel_id=1, source_target_pairs={{0,1},{1,0},{2,3},{3,2},{4,5},{5,4},{6,7},{7,6}} | collective-permute-start | bytes 6291464 | tf_op jit(solution)/shard_map/ppermute | solution.py:310
  2730.7 90.0 %collective-permute-start.7 = (f32[256,2048]{1,0:T(8,128)}, f32[256,2048]{1,0:T(8,128)}, u32[]{:S(2)}, u32[]{:S(2)}) collective-permute-start(f32[256,2048]{1,0:T(8,128)} %get-tuple-element.49), channel_id=1, source_target_pairs={{0,3},{1,2},{2,1},{3,0},{4,7},{5,6},{6,5},{7,4}} | collective-permute-start | bytes 6291464 | tf_op jit(solution)/shard_map/ppermute | solution.py:310
Sparse Core Ops, SparseCore 0:
  370.4 28.5 all-gather.16
  552.5 28.2 all-gather.18
  733.8 27.9 all-gather.8
  1105.9 27.7 all-gather.10
  1501.0 199.3 all-gather.22
  2015.6 198.9 all-gather.20
  2316.5 154.8 all-gather.14
  2836.1 155.4 all-gather.12
